TPU v7x, 8 devices: a whole 2x2x1 slice. The times are simulated.
8 devices in a mesh: dp: 1 (over z), tp: 2 (over y), ep: 4 (over x, core).
Axes of the slice: x: 2, y: 2, z: 1, core: 2. Of those that a mesh axis runs over, the one named last changes fastest.
Arguments:
- resid_in: bfloat16 [512, 7168], P(('dp', 'ep'))
- norm_scale: bfloat16 [7168], replicated
- w_router: bfloat16 [7168, 128], replicated
- w_gate: bfloat16 [128, 7168, 256], P('ep', None, 'tp')
- w_up: bfloat16 [128, 7168, 256], P('ep', None, 'tp')
- w_down: bfloat16 [128, 256, 7168], P('ep', 'tp')
- choice: int32 [512, 2], P(('dp', 'ep'))
Outputs:
- output: bfloat16 [512, 7168], P(('dp', 'ep'))
All inputs are finite; a program needn't handle non-finite values.
Results may differ from a plain program's by a relative error of at most 0.00572865.
Values are sent between devices in bfloat16 or wider.
A program may use at most 1 GiB of HBM per device.

v0:
```python
import jax
import jax.numpy as jnp
from jax import lax
from jax.sharding import PartitionSpec as P

NORM_EPS = 1e-5


def norm_route(resid_rows, norm_scale, w_router, choice_rows):
    rows_f32 = resid_rows.astype(jnp.float32)
    centered = rows_f32 - jnp.mean(rows_f32, axis=-1, keepdims=True)
    variance = jnp.mean(centered * centered, axis=-1, keepdims=True)
    normed = (centered * lax.rsqrt(variance + NORM_EPS) * norm_scale.astype(jnp.float32)).astype(jnp.bfloat16)
    logits = jnp.dot(normed, w_router, preferred_element_type=jnp.float32)
    router_probs = jax.nn.softmax(logits, axis=-1)
    expert_ids = jnp.arange(w_router.shape[1], dtype=jnp.int32)
    picked = jnp.sum(jnp.where(choice_rows[:, :, None] == expert_ids[None, None, :], router_probs[:, None, :], 0.0), axis=-1)
    gate_vals = picked / jnp.sum(picked, axis=-1, keepdims=True)
    return normed, gate_vals


def slot_table(choice_rows, experts, capacity):
    flat_ids = choice_rows.reshape(-1)
    onehot = (flat_ids[:, None] == jnp.arange(experts, dtype=jnp.int32)[None, :]).astype(jnp.int32)
    earlier = jnp.cumsum(onehot, axis=0) - onehot
    position = jnp.sum(earlier * onehot, axis=1)
    return flat_ids * capacity + position, position < capacity


def slot_sources(slot_ids, is_kept, num_slots, top_k):
    slot_match = (slot_ids[None, :] == jnp.arange(num_slots, dtype=jnp.int32)[:, None]) & is_kept[None, :]
    token_rows = jnp.arange(slot_ids.shape[0], dtype=jnp.int32) // top_k
    source_row = jnp.sum(jnp.where(slot_match, token_rows[None, :], 0), axis=1)
    return source_row, jnp.any(slot_match, axis=1)


def expert_glu(rows_in, w_gate, w_up, w_down):
    gate_act = jnp.einsum('esd,edf->esf', rows_in, w_gate, preferred_element_type=jnp.float32)
    up_act = jnp.einsum('esd,edf->esf', rows_in, w_up, preferred_element_type=jnp.float32)
    hidden = (jax.nn.silu(gate_act) * up_act).astype(jnp.bfloat16)
    return jnp.einsum('esf,efd->esd', hidden, w_down, preferred_element_type=jnp.float32).astype(jnp.bfloat16)


def solution(mesh):
    row_spec = P(('dp', 'ep'), None)

    def device_step(resid_in, norm_scale, w_router, w_gate, w_up, w_down, choice):
        tok_rows, d_model = resid_in.shape
        experts = w_router.shape[1]
        top_k = choice.shape[1]
        capacity = (2 * tok_rows * top_k + experts - 1) // experts
        normed, gate_vals = norm_route(resid_in, norm_scale, w_router, choice)
        slot_ids, is_kept = slot_table(choice, experts, capacity)
        source_row, filled = slot_sources(slot_ids, is_kept, experts * capacity, top_k)
        send_rows = jnp.where(filled[:, None], jnp.take(normed, source_row, axis=0), jnp.zeros((), jnp.bfloat16))
        send_rows = send_rows.reshape(experts, capacity, d_model)
        expert_rows = lax.all_to_all(send_rows, 'ep', 0, 1, tiled=True)
        expert_out = expert_glu(expert_rows, w_gate, w_up, w_down)
        back_rows = lax.all_to_all(expert_out, 'ep', 1, 0, tiled=True).reshape(experts * capacity, d_model)
        kept_rows = is_kept.reshape(tok_rows, top_k)
        safe_slots = jnp.where(kept_rows, slot_ids.reshape(tok_rows, top_k), 0)
        weights = jnp.where(kept_rows, gate_vals, 0.0)
        picked_rows = jnp.take(back_rows, safe_slots, axis=0)
        mixed_rows = jnp.sum(weights[:, :, None] * picked_rows, axis=1)
        tp_total = lax.psum(mixed_rows, 'tp')
        return (resid_in.astype(jnp.float32) + tp_total).astype(jnp.bfloat16)

    return jax.shard_map(device_step, mesh=mesh, in_specs=(row_spec, P(None), P(None, None), P('ep', None, 'tp'), P('ep', None, 'tp'), P('ep', 'tp', None), row_spec), out_specs=row_spec, check_vma=False)
```

profile of v0, /device:TPU:0, one launch (start us, length us, event | category | flops | bytes accessed | tf_op | source)
XLA Modules:
  0.0 499.3 jit_solution(2393384669630228364)
XLA Ops:
  6.5 0.0 copy-start
  6.5 0.0 copy-start.2
  6.5 0.9 copy.38
  7.5 0.1 eq.51
  7.6 0.1 eq.55
  7.8 0.1 copy.40
  7.9 0.2 fusion.14
  8.1 0.0 copy-start.1
  8.2 0.2 fusion.16
  8.4 1.9 convert_reduce_fusion
  10.3 0.0 copy-done.1
  10.4 0.6 fusion.2
  11.0 0.0 copy-done.2
  11.0 0.2 fusion.8
  11.2 0.2 select_reduce_fusion
  11.4 0.1 reduce_sum.86
  11.5 0.1 broadcast_in_dim.89
  11.7 3.4 fusion.4
  15.0 16.0 %gather_fusion = bf16[512,7168]{1,0:T(8,128)(2,1)} fusion(bf16[128,7168]{1,0:T(8,128)(2,1)} %fusion.4, s32[1024]{0:T(1024)S(1)} %pad_clamp_fusion.1), kind=kCustom, calls=%fused_computation | custom fusion | bytes 14682112 | tf_op jit(solution)/shard_map/jit(_take)/gather | solution.py:55
  31.0 12.6 %gather.11 = bf16[128,4,7168]{2,1,0:T(4,128)(2,1)} reshape(bf16[512,7168]{1,0:T(8,128)(2,1)} %gather_fusion) | data formatting | bytes 14680064 | tf_op jit(solution)/shard_map/jit(_take)/gather | solution.py:55
  43.7 10.0 %select_select_fusion = bf16[128,4,7168]{2,1,0:T(4,128)(2,1)} fusion(bf16[128,4,7168]{2,1,0:T(4,128)(2,1)} %gather.11, pred[128,4]{1,0:T(8,128)(4,1)S(1)} %compare_and_fusion, pred[128,4]{1,0:T(8,128)(4,1)S(1)} %broadcast_in_dim.89), kind=kLoop, calls=%fused_computation.5 | loop fusion | flops 7340032 | bytes 14681088 | tf_op jit(solution)/shard_map/jit(_where)/select_n | solution.py:55
  53.7 86.9 %all_to_all.33 = bf16[128,4,7168]{2,1,0:T(4,128)(2,1)S(1)} all-to-all(bf16[128,4,7168]{2,1,0:T(4,128)(2,1)} %select_select_fusion), channel_id=1, replica_groups=mesh['dp'=1,'tp'=2,'ep'=4] {'ep'}, dimensions={0} | all-to-all | bytes 14680064 | tf_op jit(solution)/shard_map/all_to_all | solution.py:57
  140.6 5.2 %copy.47 = bf16[128,4,7168]{2,0,1:T(8,128)(2,1)} copy(bf16[128,4,7168]{2,1,0:T(4,128)(2,1)S(1)} %all_to_all.33) | data formatting | bytes 14680064 | tf_op jit(solution)/shard_map/all_to_all | solution.py:57
  145.8 11.7 %copy.48 = bf16[32,4,4,7168]{3,2,1,0:T(4,128)(2,1)} copy(bf16[32,4,4,7168]{3,0,1,2:T(8,128)(2,1)} %bitcast.37) | data formatting | bytes 14680064 | tf_op jit(solution)/shard_map/all_to_all | solution.py:57
  157.5 12.1 %all_to_all.27 = bf16[32,16,7168]{2,1,0:T(8,128)(2,1)} reshape(bf16[32,4,4,7168]{3,2,1,0:T(4,128)(2,1)} %copy.48) | data formatting | bytes 14680064 | tf_op jit(solution)/shard_map/all_to_all | solution.py:57
  169.6 22.8 %fusion.24 = f32[32,16,128]{2,1,0:T(8,128)S(1)} fusion(bf16[32,16,7168]{2,1,0:T(8,128)(2,1)} %all_to_all.27, bf16[32,7168,128]{2,1,0:T(8,128)(2,1)} %param.10), kind=kOutput, calls=%fused_computation.63 | convolution fusion | flops 939524096 | bytes 66322432 | tf_op jit(solution)/shard_map/esd,edf->esf/dot_general | solution.py:38
  192.4 23.3 %fusion.6.clone.4 = bf16[32,16,128]{2,1,0:T(8,128)(2,1)S(1)} fusion(bf16[32,16,7168]{2,1,0:T(8,128)(2,1)} %all_to_all.27, bf16[32,7168,128]{2,1,0:T(8,128)(2,1)} %param.11, f32[32,16,128]{2,1,0:T(8,128)S(1)} %fusion.24), kind=kOutput, calls=%fused_computation.17.clone.clone.clone.1 | convolution fusion | flops 939917312 | bytes 66453504 | tf_op jit(solution)/shard_map/esd,edf->esf/dot_general | solution.py:39
  215.7 24.0 %convolution_convert_fusion = bf16[32,16,7168]{2,1,0:T(8,128)(2,1)} fusion(bf16[32,128,7168]{2,1,0:T(8,128)(2,1)} %param.12, bf16[32,16,128]{2,1,0:T(8,128)(2,1)S(1)} %fusion.6.clone.4), kind=kOutput, calls=%fused_computation.2 | convolution fusion | flops 943194112 | bytes 66191360 | tf_op jit(solution)/shard_map/esf,efd->esd/dot_general | solution.py:41
  239.7 10.1 %copy.49 = bf16[32,16,7168]{2,0,1:T(8,128)(2,1)} copy(bf16[32,16,7168]{2,1,0:T(8,128)(2,1)} %convolution_convert_fusion) | data formatting | bytes 14680064 | tf_op jit(solution)/shard_map/convert_element_type | solution.py:41
  249.9 0.0 copy-start.3
  249.9 5.6 %all-to-all-start.1 = ((bf16[32,16,7168]{2,0,1:T(8,128)(2,1)}), bf16[32,16,7168]{2,0,1:T(8,128)(2,1)}, u32[]{:S(2)}, u32[]{:S(2)}) async-start(bf16[32,16,7168]{2,0,1:T(8,128)(2,1)} %copy.49), calls=%async_computation.1 | async-start | bytes 14680064 | tf_op jit(solution)/shard_map/all_to_all | solution.py:59
  255.4 0.4 all-reduce.2.cloned.1.call-start
  255.9 0.1 reduce_sum.79
  256.0 0.1 copy.42
  256.1 0.0 copy-done.3
  256.1 0.1 copy.46
  256.3 0.1 copy.51
  256.4 0.1 reshape.139
  256.5 0.0 copy-done
  256.5 2.3 fusion.23
  259.0 0.1 copy.43
  259.1 0.2 select_reduce_fusion.1
  259.3 0.1 copy.44
  259.4 77.6 %all-to-all-done.1 = bf16[32,16,7168]{2,0,1:T(8,128)(2,1)} async-done(((bf16[32,16,7168]{2,0,1:T(8,128)(2,1)}), bf16[32,16,7168]{2,0,1:T(8,128)(2,1)}, u32[]{:S(2)}, u32[]{:S(2)}) %all-to-all-start.1) | async-done | bytes 7340064 | tf_op jit(solution)/shard_map/all_to_all | solution.py:59
  337.0 11.8 %copy.53 = bf16[32,4,4,7168]{3,2,0,1:T(4,128)(2,1)} copy(bf16[32,4,4,7168]{3,0,2,1:T(8,128)(2,1)} %bitcast.7) | data formatting | bytes 14680064 | tf_op jit(solution)/shard_map/all_to_all | solution.py:59
  348.8 12.3 %reshape.128 = bf16[512,7168]{1,0:T(8,128)(2,1)} reshape(bf16[4,32,4,7168]{3,2,1,0:T(4,128)(2,1)} %bitcast.38) | data formatting | bytes 14680064 | tf_op jit(solution)/shard_map/reshape | solution.py:59
  361.1 12.1 %gather_fusion.1 = bf16[256,7168]{1,0:T(8,128)(2,1)} fusion(bf16[512,7168]{1,0:T(8,128)(2,1)} %reshape.128, s32[1024]{0:T(1024)S(1)} %pad_clamp_fusion), kind=kCustom, calls=%fused_computation.1 | custom fusion | bytes 7341056 | tf_op jit(solution)/shard_map/jit(_take)/gather | solution.py:63
  373.2 8.1 %reshape.138 = bf16[128,2,7168]{2,1,0:T(2,128)(2,1)} reshape(bf16[256,7168]{1,0:T(8,128)(2,1)} %gather_fusion.1) | data formatting | bytes 7340032 | tf_op jit(solution)/shard_map/jit(_take)/gather | solution.py:63
  381.3 14.4 %multiply_reduce_fusion = f32[128,7168]{1,0:T(8,128)} fusion(bf16[128,2,7168]{2,1,0:T(2,128)(2,1)} %reshape.138, pred[128,2]{1,0:T(8,128)(4,1)S(1)} %copy.46, f32[128,2]{1,0:T(8,128)S(1)} %copy.44), kind=kLoop, calls=%fused_computation.4 | loop fusion | flops 6422528 | bytes 7341312 | tf_op jit(solution)/shard_map/reduce_sum | solution.py:64
  395.7 0.0 all-reduce.2.cloned.1.call-update
  395.7 92.4 %all-reduce.2.cloned.1.call-done = f32[128,7168]{1,0:T(8,128)} async-done(((f32[128,7168]{1,0:T(8,128)}), f32[128,7168]{1,0:T(8,128)}) %all-reduce.2.cloned.1.call-update) | async-done | bytes 3670032 | tf_op jit(solution)/shard_map/psum | solution.py:65
  488.1 4.2 fusion.5
  (19 shorter events, 0.2 us)
Async XLA Ops:
  6.5 250.0 %copy-start = (bf16[7168,128]{1,0:T(8,128)(2,1)S(1)}, bf16[7168,128]{1,0:T(8,128)(2,1)}, u32[]{:S(2)}) copy-start(bf16[7168,128]{1,0:T(8,128)(2,1)} %param.9) | copy-start | bytes 5505028
  6.5 4.5 copy-start.2
  8.1 2.2 copy-start.1
  249.9 6.2 %copy-start.3 = (s32[128,2]{0,1:T(2,128)S(1)}, s32[128,2]{0,1:T(2,128)}, u32[]{:S(2)}) copy-start(s32[128,2]{0,1:T(2,128)} %param.13) | copy-start | bytes 3076
  249.9 87.2 %all-to-all-start.1 = ((bf16[32,16,7168]{2,0,1:T(8,128)(2,1)}), bf16[32,16,7168]{2,0,1:T(8,128)(2,1)}, u32[]{:S(2)}, u32[]{:S(2)}) async-start(bf16[32,16,7168]{2,0,1:T(8,128)(2,1)} %copy.49), calls=%async_computation.1 | async-start | bytes 14680064 | tf_op jit(solution)/shard_map/all_to_all | solution.py:59
  255.4 232.7 %all-reduce.2.cloned.1.call-start = ((), (), s32[]{:S(2)}) async-start(), calls=%async_computation.2 | async-start | bytes 7340032 | tf_op jit(solution)/shard_map/psum | solution.py:65
Sparse Core Ops, SparseCore 0:
  395.9 92.2 all-reduce.1
where the time goes:
time: 504 us; the launch traced here: 499 us
  waiting for transfers between devices  170 us (34%)
  local copies, waits for them, and re-layouts  114 us (23%)
  blocking collectives  86.9 us (17%)
  matrix products  72.5 us (14%)
  other arithmetic  35.7 us (7%)
  between operations  13.8 us (3%)
  starting transfers between devices  6.02 us (1%)
    psum x1, waiting for transfers between devices, device_step(): tp_total = lax.psum(mixed_rows, 'tp')  92.4 us
    all_to_all x1, blocking collectives, device_step(): expert_rows = lax.all_to_all(send_rows, 'ep', 0, 1, tiled=True)  86.9 us
    all_to_all x1, waiting for transfers between devices, device_step(): lax.all_to_all(expert_out, 'ep', 1, 0, tiled=True)  77.6 us
    all_to_all x3, local copies, waits for them, and re-layouts, device_step(): expert_rows = lax.all_to_all(send_rows, 'ep', 0, 1, tiled=True)  29 us
    gather x2, local copies, waits for them, and re-layouts, device_step(): jnp.take(normed, source_row, axis=0)  28.6 us
    dot_general x1, matrix products, expert_glu(): jnp.einsum('esf,efd->esd', hidden, w_down, preferred_element_type=jnp.flo...  24 us
    dot_general x1, matrix products, expert_glu(): jnp.einsum('esd,edf->esf', rows_in, w_up, preferred_element_type=jnp.floa...  23.3 us
    dot_general x1, matrix products, expert_glu(): jnp.einsum('esd,edf->esf', rows_in, w_gate, preferred_element_type=jnp.fl...  22.8 us
  transfers between devices with their start and end apart: 2, of which 2 were waited for; matrix products, arithmetic and copies ran while one was open for 1% of the time, Pallas kernels for 0%

commit v1 on v0

v1 whole, which is shorter than its diff:
```python
import functools

import jax
import jax.numpy as jnp
from jax import lax
from jax.experimental import pallas as pl
from jax.experimental.pallas import tpu as pltpu
from jax.sharding import PartitionSpec as P

NORM_EPS = 1e-5
MESH = pl.DeviceIdType.MESH
F32 = jnp.float32
BF16 = jnp.bfloat16
CAP = 4
GROUPS = 4
UP_STEPS = 14
UP_BUFS = 4
DOWN_STEPS = 7
DOWN_BUFS = 3
VMEM_LIMIT = 62 * 1024 * 1024


def remote(src, dst, send_sem, recv_sem, device):
    return pltpu.make_async_remote_copy(src_ref=src, dst_ref=dst, send_sem=send_sem, recv_sem=recv_sem, device_id=device, device_id_type=MESH)


def place():
    dp, tp, ep = lax.axis_index('dp'), lax.axis_index('tp'), lax.axis_index('ep')
    return dp, tp, ep, ep // 2, ep % 2


def up_kernel(x_ref, g_ref, wr_hbm, wg_hbm, wu_hbm, tok_ref, choice_ref, hid_ref, gate_ref,
              u_ref, xs_ref, pick_ref, acc_ref, wbuf, wr_ref, logit_ref,
              w_sem, wr_sem, own_s, own_r, x_s, x_r, y_s, y_r, dx_s, dx_r, dy_s, dy_r):
    dp, tp, ep, cx, core = place()
    local = wg_hbm.shape[0]
    tok, d_model = x_ref.shape
    half = d_model // 2
    steps = UP_STEPS
    cw = half // steps
    twin = (dp, tp, cx * 2 + (1 - core))
    across = (dp, tp, (1 - cx) * 2 + core)
    other_tp = (dp, 1 - tp, ep)
    far = (1 - cx) * 2 + core

    barrier = pltpu.get_barrier_semaphore()
    for peer in (twin, across, other_tp):
        pl.semaphore_signal(barrier, inc=1, device_id=peer, device_id_type=MESH)

    def weight_copies(step, slot):
        out = []
        for h in range(2):
            rows = pl.ds(pl.multiple_of(h * half + step * cw, cw), cw)
            for m, w in enumerate((wg_hbm, wu_hbm)):
                out.append(pltpu.make_async_copy(w.at[:, rows, :], wbuf.at[slot, :, h * cw:(h + 1) * cw, m * 128:(m + 1) * 128], w_sem.at[slot, h * 2 + m]))
        return out

    wr_copy = pltpu.make_async_copy(wr_hbm, wr_ref, wr_sem)
    for c in weight_copies(0, 0):
        c.start()
    wr_copy.start()
    for b in range(1, UP_BUFS):
        for c in weight_copies(b, b):
            c.start()

    def norm_rows(r, carry):
        rows = pl.ds(pl.multiple_of(r * 16, 16), 16)
        xb = x_ref[rows, :].astype(F32)
        cen = xb - jnp.mean(xb, axis=-1, keepdims=True)
        var = jnp.mean(cen * cen, axis=-1, keepdims=True)
        u = (cen * lax.rsqrt(var + NORM_EPS) * g_ref[...].astype(F32)).astype(BF16)
        for j in range(steps):
            for h in range(2):
                u_ref[j, h, ep, rows, :] = u[:, h * half + j * cw:h * half + (j + 1) * cw]
        return carry

    lax.fori_loop(0, tok // 16, norm_rows, 0)
    slots = tok_ref.shape[0]
    pick_ref[...] = jnp.where(tok_ref[...] == lax.broadcasted_iota(jnp.int32, (slots, GROUPS * tok), 1), 1.0, 0.0).astype(BF16)
    acc_ref[...] = jnp.zeros_like(acc_ref)
    logit_ref[...] = jnp.zeros_like(logit_ref)
    pl.semaphore_wait(barrier, 3)

    def own_copy(j):
        return remote(u_ref.at[j, :, ep], u_ref.at[j, :, ep], own_s.at[j], own_r.at[j], twin)

    def x_copy(j):
        return remote(u_ref.at[j, tp, ep], u_ref.at[j, tp, ep], x_s.at[j], x_r.at[j], across)

    def y_copy(j):
        return remote(u_ref.at[j, tp, far], u_ref.at[j, tp, far], y_s.at[j], y_r.at[j], other_tp)

    def dx_copy(j):
        return remote(u_ref.at[j, tp, far], u_ref.at[j, tp, far], dx_s.at[j], dx_r.at[j], twin)

    def dy_copy(j):
        return remote(u_ref.at[j, 1 - tp, far], u_ref.at[j, 1 - tp, far], dy_s.at[j], dy_r.at[j], twin)

    def first_sends(j, carry):
        x_copy(j).start()
        own_copy(j).start()
        return carry

    lax.fori_loop(0, steps, first_sends, 0)
    wr_copy.wait()

    def main(i, carry):
        @pl.when(i < steps)
        def _():
            x_copy(i).wait_recv()
            y_copy(i).start()
            dx_copy(i).start()

        @pl.when((i >= 1) & (i < steps + 1))
        def _():
            j = i - 1
            y_copy(j).wait_recv()
            dy_copy(j).start()

        @pl.when(i >= 2)
        def _():
            j = i - 2
            slot = lax.rem(j, UP_BUFS)
            for h in range(2):
                kr = pl.ds(pl.multiple_of(h * half + j * cw, cw), cw)
                logit_ref[...] += jnp.dot(u_ref[j, h, ep], wr_ref[kr, :], preferred_element_type=F32)
            own_copy(j).wait_recv()
            dx_copy(j).wait_recv()
            dy_copy(j).wait_recv()
            for h in range(2):
                block = u_ref[j, h].reshape(GROUPS * tok, cw)
                xs_ref[:, h * cw:(h + 1) * cw] = jnp.dot(pick_ref[...], block, preferred_element_type=F32).astype(BF16)
            for c in weight_copies(j, slot):
                c.wait()

            def experts(t, carry2):
                for z in range(4):
                    e = t * 4 + z
                    rows = pl.ds(pl.multiple_of(e * 16, 16), 16)
                    acc_ref[rows, :] += jnp.dot(xs_ref[rows, :], wbuf[slot, e], preferred_element_type=F32)
                return carry2

            lax.fori_loop(0, local // 4, experts, 0)

            @pl.when(j + UP_BUFS < steps)
            def _():
                for c in weight_copies(j + UP_BUFS, slot):
                    c.start()
        return carry

    lax.fori_loop(0, steps + 2, main, 0)

    gate_act = acc_ref[:, :128]
    hid_ref[...] = (gate_act * jax.nn.sigmoid(gate_act) * acc_ref[:, 128:]).astype(BF16)
    logits = logit_ref[...]
    ex = jnp.exp(logits - jnp.max(logits, axis=-1, keepdims=True))
    probs = ex / jnp.sum(ex, axis=-1, keepdims=True)
    ids = lax.broadcasted_iota(jnp.int32, probs.shape, 1)
    p0 = jnp.sum(jnp.where(choice_ref[:, 0:1] == ids, probs, 0.0), axis=-1, keepdims=True)
    p1 = jnp.sum(jnp.where(choice_ref[:, 1:2] == ids, probs, 0.0), axis=-1, keepdims=True)
    gate_ref[:, 0:1] = p0 / (p0 + p1)
    gate_ref[:, 1:2] = p1 / (p0 + p1)

    def last_waits(j, carry):
        x_copy(j).wait_send()
        own_copy(j).wait_send()
        y_copy(j).wait_send()
        dx_copy(j).wait_send()
        dy_copy(j).wait_send()
        return carry

    lax.fori_loop(0, steps, last_waits, 0)


def down_kernel(rows_c, rows_n, hid_ref, x_ref, gate_ref, slotkey_ref, keycol_ref, keyrow_ref, nkey_ref, poskey_ref, npos_ref, wd_hbm, out_ref,
                send_ref, land_ref, fwd_ref, yland_ref, qs_ref, w2buf, p_ref, s_ref, a_ref, b_ref,
                w_sem, q_s, q_r, f_s, f_r, o_s, o_r):
    dp, tp, ep, cx, core = place()
    local = wd_hbm.shape[0]
    tok, d_model = x_ref.shape
    half = d_model // 2
    steps = DOWN_STEPS
    cw = half // steps
    peers = [(1 - cx) * 2 + core, (1 - cx) * 2 + (1 - core), cx * 2 + (1 - core)]
    other_tp = (dp, 1 - tp, ep)

    barrier = pltpu.get_barrier_semaphore()
    for g in peers:
        pl.semaphore_signal(barrier, inc=1, device_id=(dp, tp, g), device_id_type=MESH)
    pl.semaphore_signal(barrier, inc=1, device_id=other_tp, device_id_type=MESH)

    def weight_copies(step, slot):
        out = []
        for h in range(2):
            cols = pl.ds(pl.multiple_of(h * half + step * cw, 128), cw)
            out.append(pltpu.make_async_copy(wd_hbm.at[:, :, cols], w2buf.at[slot, :, :, h * cw:(h + 1) * cw], w_sem.at[slot, h]))
        return out

    for b in range(DOWN_BUFS):
        for c in weight_copies(b, b):
            c.start()

    p_ref[...] = jnp.where(keycol_ref[...] == slotkey_ref[...], 1.0, 0.0).astype(BF16)
    s_ref[...] = jnp.where(lax.broadcasted_iota(jnp.int32, s_ref.shape, 0) == nkey_ref[...], 1.0, 0.0).astype(BF16)

    def split_gates(keys, pos, dst):
        mat = jnp.where(pos[:, 0:1] == keys, gate_ref[:, 0:1], 0.0) + jnp.where(pos[:, 1:2] == keys, gate_ref[:, 1:2], 0.0)
        for z in range(3):
            part = mat.astype(BF16)
            dst[z] = part
            mat = mat - part.astype(F32)

    split_gates(keyrow_ref[...], poskey_ref[...], a_ref)
    split_gates(lax.broadcasted_iota(jnp.int32, (tok, rows_n), 1), npos_ref[...], b_ref)
    pl.semaphore_wait(barrier, 4)

    def q_copy(k, n):
        return remote(send_ref.at[k, :, peers[n]], land_ref.at[k, :, ep], q_s.at[k, n], q_r.at[k, n], (dp, tp, peers[n]))

    def f_copy(k):
        return remote(fwd_ref.at[k], yland_ref.at[k], f_s.at[k], f_r.at[k], other_tp)

    def o_copy(k):
        cols = pl.ds(pl.multiple_of(tp * half + k * cw, 128), cw)
        return remote(out_ref.at[:, cols], out_ref.at[:, cols], o_s.at[k], o_r.at[k], other_tp)

    def main(i, carry):
        @pl.when(i < steps)
        def _():
            slot = lax.rem(i, DOWN_BUFS)
            for c in weight_copies(i, slot):
                c.wait()

            def experts(t, carry2):
                for z in range(4):
                    e = t * 4 + z
                    rows = pl.ds(pl.multiple_of(e * 16, 16), 16)
                    qs_ref[rows, :] = jnp.dot(hid_ref[rows, :], w2buf[slot, e], preferred_element_type=F32).astype(BF16)
                return carry2

            lax.fori_loop(0, local // 4, experts, 0)
            for h in range(2):
                send_ref[i, h] = jnp.dot(p_ref[...], qs_ref[:, h * cw:(h + 1) * cw], preferred_element_type=F32).astype(BF16).reshape(GROUPS, rows_c, cw)
            land_ref[i, :, ep] = send_ref[i, :, ep]

            @pl.when(i + DOWN_BUFS < steps)
            def _():
                for c in weight_copies(i + DOWN_BUFS, slot):
                    c.start()
            for n in range(3):
                q_copy(i, n).start()

        @pl.when((i >= 1) & (i < steps + 1))
        def _():
            k = i - 1
            for n in range(3):
                q_copy(k, n).wait_recv()
            block = land_ref[k, 1 - tp].reshape(GROUPS * rows_c, cw)
            fwd_ref[k] = jnp.dot(s_ref[...], block, preferred_element_type=F32).astype(BF16)
            f_copy(k).start()

        @pl.when(i >= 2)
        def _():
            k = i - 2
            mine = land_ref[k, tp].reshape(GROUPS * rows_c, cw)
            mix = jnp.dot(a_ref[2], mine, preferred_element_type=F32)
            mix += jnp.dot(a_ref[1], mine, preferred_element_type=F32)
            mix += jnp.dot(a_ref[0], mine, preferred_element_type=F32)
            f_copy(k).wait_recv()
            theirs = yland_ref[k]
            for z in (2, 1, 0):
                mix += jnp.dot(b_ref[z], theirs, preferred_element_type=F32)
            cols = pl.ds(pl.multiple_of(tp * half + k * cw, 128), cw)
            out_ref[:, cols] = (x_ref[:, cols].astype(F32) + mix).astype(BF16)
            o_copy(k).start()
        return carry

    lax.fori_loop(0, steps + 2, main, 0)

    def last_waits(k, carry):
        for n in range(3):
            q_copy(k, n).wait_send()
        f_copy(k).wait_send()
        o_copy(k).wait_send()
        cols = pl.ds(pl.multiple_of((1 - tp) * half + k * cw, 128), cw)
        remote(out_ref.at[:, cols], out_ref.at[:, cols], o_s.at[k], o_r.at[k], other_tp).wait_recv()
        return carry

    lax.fori_loop(0, steps, last_waits, 0)


def routing(choice):
    ep = lax.axis_index('ep')
    pairs = choice.shape[0] * choice.shape[1]
    ids = lax.all_gather(choice, 'ep', tiled=True).reshape(GROUPS, pairs)
    onehot = (ids[:, :, None] == jnp.arange(128, dtype=jnp.int32)).astype(BF16)
    order = jnp.arange(pairs, dtype=jnp.int32)
    tri = (order[:, None] > order[None, :]).astype(BF16)
    earlier = jnp.einsum('pq,gqe->gpe', tri, onehot, preferred_element_type=F32)
    position = jnp.sum(earlier * onehot.astype(F32), axis=-1).astype(jnp.int32)
    kept = position < CAP
    owner = ids // 32
    hot = ((owner[:, :, None] == jnp.arange(GROUPS, dtype=jnp.int32)) & kept[:, :, None])
    hot = jnp.concatenate([hot, kept[:, :, None]], axis=-1).astype(BF16)
    before = jnp.einsum('pq,gqe->gpe', tri, hot, preferred_element_type=F32)
    rank = jnp.sum((before * hot.astype(F32))[:, :, :GROUPS], axis=-1).astype(jnp.int32)
    nrank = before[:, :, GROUPS].astype(jnp.int32)
    count = jnp.sum(hot.astype(F32), axis=1).astype(jnp.int32)
    max_c = jnp.max(count[:, :GROUPS])
    max_n = jnp.max(count[:, GROUPS])
    group = jnp.arange(GROUPS, dtype=jnp.int32)[:, None]
    slot = jnp.where(kept & (owner == ep), (ids - ep * 32) * 16 + group * CAP + position, -1).reshape(-1)
    token = (group * (pairs // 2) + order[None, :] // 2).reshape(-1)
    match = slot[None, :] == jnp.arange(512, dtype=jnp.int32)[:, None]
    tok_of = jnp.max(jnp.where(match, token[None, :], -1), axis=1)
    slotkey = jnp.max(jnp.where(match, (group * 128 + rank).reshape(-1)[None, :], -1), axis=1)
    key = jnp.where(kept, owner * 128 + rank, -1)
    npos = jnp.where(kept, nrank, -1)
    my_key = lax.dynamic_index_in_dim(key, ep, 0, keepdims=False)
    my_n = lax.dynamic_index_in_dim(npos, ep, 0, keepdims=False)
    nkey = jnp.max(jnp.where(my_key[None, :] == jnp.arange(512, dtype=jnp.int32)[:, None], my_n[None, :], -1), axis=1)
    return tok_of[:, None], slotkey[None, :], my_key.reshape(-1, 2), my_n.reshape(-1, 2), nkey.reshape(GROUPS, 128), max_c, max_n


def run_up(x, g, wr, wg, wu, tok_of, choice):
    tok, d_model = x.shape
    local = wg.shape[0]
    cw = d_model // 2 // UP_STEPS
    slots = tok_of.shape[0]
    vm = pl.BlockSpec(memory_space=pltpu.VMEM)
    hbm = pl.BlockSpec(memory_space=pl.ANY)
    sem = pltpu.SemaphoreType.DMA
    return pl.pallas_call(
        up_kernel,
        out_shape=(jax.ShapeDtypeStruct((slots, 128), BF16), jax.ShapeDtypeStruct((tok, 2), F32)),
        in_specs=[vm, vm, hbm, hbm, hbm, vm, vm],
        out_specs=(vm, vm),
        scratch_shapes=[
            pltpu.VMEM((UP_STEPS, 2, GROUPS, tok, cw), BF16),
            pltpu.VMEM((slots, 2 * cw), BF16),
            pltpu.VMEM((slots, GROUPS * tok), BF16),
            pltpu.VMEM((slots, 256), F32),
            pltpu.VMEM((UP_BUFS, local, 2 * cw, 256), BF16),
            pltpu.VMEM(wr.shape, BF16),
            pltpu.VMEM((tok, 128), F32),
            sem((UP_BUFS, 4)), sem,
        ] + [sem((UP_STEPS,))] * 10,
        compiler_params=pltpu.CompilerParams(collective_id=0, has_side_effects=True, vmem_limit_bytes=VMEM_LIMIT),
        name='up',
    )(x, g, wr, wg, wu, tok_of, choice)


def run_down(tier, rows_c, rows_n, hid, x, gate, slotkey, poskey, npos, nkey, wd):
    tok, d_model = x.shape
    local = wd.shape[0]
    cw = d_model // 2 // DOWN_STEPS
    slots = hid.shape[0]
    keys = (jnp.arange(GROUPS, dtype=jnp.int32)[:, None] * 128 + jnp.arange(rows_c, dtype=jnp.int32)[None, :]).reshape(-1)
    nkey = nkey[:, :rows_c].reshape(1, -1)
    vm = pl.BlockSpec(memory_space=pltpu.VMEM)
    hbm = pl.BlockSpec(memory_space=pl.ANY)
    sem = pltpu.SemaphoreType.DMA
    return pl.pallas_call(
        functools.partial(down_kernel, rows_c, rows_n),
        out_shape=jax.ShapeDtypeStruct(x.shape, BF16),
        in_specs=[vm] * 9 + [hbm],
        out_specs=vm,
        scratch_shapes=[
            pltpu.VMEM((DOWN_STEPS, 2, GROUPS, rows_c, cw), BF16),
            pltpu.VMEM((DOWN_STEPS, 2, GROUPS, rows_c, cw), BF16),
            pltpu.VMEM((DOWN_STEPS, rows_n, cw), BF16),
            pltpu.VMEM((DOWN_STEPS, rows_n, cw), BF16),
            pltpu.VMEM((slots, 2 * cw), BF16),
            pltpu.VMEM((DOWN_BUFS, local, 128, 2 * cw), BF16),
            pltpu.VMEM((GROUPS * rows_c, slots), BF16),
            pltpu.VMEM((rows_n, GROUPS * rows_c), BF16),
            pltpu.VMEM((3, tok, GROUPS * rows_c), BF16),
            pltpu.VMEM((3, tok, rows_n), BF16),
            sem((DOWN_BUFS, 2)), sem((DOWN_STEPS, 3)), sem((DOWN_STEPS, 3)),
            sem((DOWN_STEPS,)), sem((DOWN_STEPS,)), sem((DOWN_STEPS,)), sem((DOWN_STEPS,)),
        ],
        compiler_params=pltpu.CompilerParams(collective_id=1 + tier, has_side_effects=True, vmem_limit_bytes=VMEM_LIMIT),
        name='down%d' % rows_c,
    )(hid, x, gate, slotkey, keys[:, None], keys[None, :], nkey, poskey, npos, wd)


def solution(mesh):
    row_spec = P(('dp', 'ep'), None)

    def device_step(resid_in, norm_scale, w_router, w_gate, w_up, w_down, choice):
        tok_of, slotkey, poskey, npos, nkey, max_c, max_n = routing(choice)
        hid, gate = run_up(resid_in, norm_scale[None, :], w_router, w_gate, w_up, tok_of, choice)
        args = (hid, resid_in, gate, slotkey, poskey, npos, nkey, w_down)
        small = (max_c <= 64) & (max_n <= 176)
        return lax.cond(small, functools.partial(run_down, 0, 64, 176), functools.partial(run_down, 1, 128, 256), *args)

    return jax.shard_map(device_step, mesh=mesh, in_specs=(row_spec, P(None), P(None, None), P('ep', None, 'tp'), P('ep', None, 'tp'), P('ep', 'tp', None), row_spec), out_specs=row_spec, check_vma=False)
```

time: 504 us -> 151 us (0.30)
  waiting for transfers between devices: 170 us -> 0 us
  Pallas kernels: 0 us -> 120 us
  local copies, waits for them, and re-layouts: 114 us -> 10.5 us
  blocking collectives: 86.9 us -> 9.94 us
  matrix products: 72.5 us -> 0.47 us
  other arithmetic: 35.7 us -> 8.23 us
  between operations: 13.8 us -> 1.52 us
  starting transfers between devices: 6.02 us -> 0 us
    pallas_call x0 -> x2, Pallas kernels: none -> 120 us  [the longest x1 64.4 us: run_down(): pl.pallas_call(functools.partial(down_kernel, rows_c, rows_n), out_shape=...]
    psum x1 -> x0, waiting for transfers between devices: 92.4 us -> none  [device_step(): tp_total = lax.psum(mixed_rows, 'tp')]
    all_to_all x1 -> x0, blocking collectives: 86.9 us -> none  [device_step(): expert_rows = lax.all_to_all(send_rows, 'ep', 0, 1, tiled=True)]
    all_to_all x1 -> x0, waiting for transfers between devices: 77.6 us -> none  [device_step(): lax.all_to_all(expert_out, 'ep', 1, 0, tiled=True)]
    dot_general x4 -> x2, matrix products: 72.5 us -> 0.47 us  [the longest x1 0.3 us: routing(): earlier = jnp.einsum('pq,gqe->gpe', tri, onehot, preferred_element_type=F32)]
    gather x4 -> x0, local copies, waits for them, and re-layouts: 48.9 us -> none  [the longest x2 28.6 us: device_step(): jnp.take(normed, source_row, axis=0)]
    all_to_all x4 -> x0, local copies, waits for them, and re-layouts: 40.8 us -> none  [the longest x3 29 us: device_step(): expert_rows = lax.all_to_all(send_rows, 'ep', 0, 1, tiled=True)]
    reduce_sum x7 -> x2, other arithmetic: 17.6 us -> 0.12 us  [the longest x1 0.1 us: routing(): count = jnp.sum(hot.astype(F32), axis=1).astype(jnp.int32)]
  transfers between devices with their start and end apart: 2 -> 0, of which waited for: 2 -> 0; matrix products, arithmetic and copies ran while one was open for 1% -> 0% of each run, Pallas kernels for 0% -> 0%
where the time goes in v1:
time: 151 us
  Pallas kernels  120 us (79%)
  local copies, waits for them, and re-layouts  10.5 us (7%)
  blocking collectives  9.94 us (7%)
  other arithmetic  8.23 us (5%)
  between operations  1.52 us (1%)
    pallas_call x1, Pallas kernels, run_down(): pl.pallas_call(functools.partial(down_kernel, rows_c, rows_n), out_shape=...  64.4 us
    pallas_call x1, Pallas kernels, run_up(): pl.pallas_call(up_kernel, out_shape=(jax.ShapeDtypeStruct((slots, 128), B...  56 us
    all_gather x1, blocking collectives, routing(): ids = lax.all_gather(choice, 'ep', tiled=True).reshape(GROUPS, pairs)  9.94 us
    unnamed x21, local copies, waits for them, and re-layouts  3.33 us

profile of v1, /device:TPU:0, one launch (start us, length us, event | category | flops | bytes accessed | tf_op | source)
XLA Modules:
  0.0 151.1 jit_solution(6564659868470956121)
XLA Ops:
  0.0 0.0 copy-start
  0.0 0.0 copy-start.6
  0.0 0.1 add_bitcast_fusion.2
  0.1 0.1 broadcast_bitcast_fusion
  0.2 9.9 %all_gather.3 = s32[512,2]{0,1:T(2,128)S(1)} all-gather(s32[128,2]{0,1:T(2,128)} %param.15), channel_id=1, replica_groups=mesh['dp'=1,'tp'=2,'ep'=4] {'ep'}, dimensions={0}, use_global_device_ids=true | all-gather | bytes 5120 | tf_op jit(solution)/shard_map/all_gather | solution.py:295
  10.1 1.3 broadcast_in_dim.65.g_ref
  11.4 1.4 copy.41.choice_ref
  12.8 0.1 copy.36
  13.0 0.2 reshape.291
  13.2 0.2 reshape.292
  13.3 0.3 fusion.1
  13.7 0.6 add_select_fusion.2
  14.3 1.0 select_reduce_fusion.4
  15.4 0.1 fusion.9
  15.5 0.7 slice_reduce_fusion
  16.9 0.6 slice_reduce_fusion.1
  18.1 0.2 convolution_bitcast_fusion.1
  18.4 0.0 copy-start.1
  18.4 0.6 copy-done.1
  19.0 0.6 dynamic-slice_select_fusion
  19.6 0.0 copy-done.6
  19.6 0.9 copy.40.tok_ref
  20.5 0.0 copy-done
  20.5 56.0 %up.1 = (bf16[512,128]{1,0:T(8,128)(2,1)S(1)}, f32[128,2]{1,0:T(8,128)S(1)}) custom-call(bf16[128,7168]{1,0:T(8,128)(2,1)S(1)} %copy-done, bf16[1,7168]{1,0:T(2,128)(2,1)} %broadcast_in_dim.65.g_ref, bf16[7168,128]{1,0:T(8,128)(2,1)} %wr_hbm.1, bf16[32,7168,128]{2,1,0:T(8,128)(2,1)} %wg_hbm.1, bf16[32,7168,128]{2,1,0:T(8,128)(2,1)} %wu_hbm.1, ...), custom_call_target="tpu_custom_call" | custom-call | tf_op jit(solution)/shard_map/up/pallas_call | solution.py:333
  76.5 0.0 copy-start.2
  76.5 0.0 copy-start.3
  76.5 0.0 copy-start.4
  76.5 0.0 copy-start.7
  76.5 1.0 iota_compare_fusion
  77.6 0.2 broadcast_in_dim.67
  77.8 0.0 copy-done.2
  77.8 0.0 copy-done.3
  77.8 0.0 copy-done.4
  77.8 0.0 copy-done.7
  77.8 72.0 %conditional.1 = (bf16[128,7168]{1,0:T(8,128)(2,1)S(1)}) conditional(s32[]{:T(128)} %convert_element_type.59, (s32[1,256]{1,0:T(1,128)S(1)}, bf16[512,128]{1,0:T(8,128)(2,1)S(1)}, bf16[128,7168]{1,0:T(8,128)(2,1)}, f32[128,2]{1,0:T(8,128)S(1)}, pred[512,1024]{1,0:T(8,128)(4,1)S(1)}, /*index=5*/s32[1,256]{1,0:T(1,128)S(1)}, ...), branch_computations={%region_8.9_spmd.clone, %region_9.10_spmd.clone} | conditional | flops 1442308 | bytes 3194992 | solution.py:395
  77.9 0.0 copy-start.8
  77.9 0.6 broadcast.207
  78.5 0.7 reduce.15
  79.2 0.7 reduce.16
  79.9 0.1 iota_add_fusion.1
  80.0 0.0 copy-done.8
  80.0 0.7 add.187.keyrow_ref
  80.6 0.1 select_reduce_fusion.3
  80.8 0.6 reshape.302.nkey_ref
  81.4 0.7 add_bitcast_fusion.1
  82.2 1.0 select_reduce_fusion.2
  83.1 0.8 reshape.304.npos_ref
  83.9 0.8 reshape.303.poskey_ref
  84.7 0.8 add.191.keycol_ref
  85.5 64.4 %down64.1 = bf16[128,7168]{1,0:T(8,128)(2,1)S(1)} custom-call(bf16[512,128]{1,0:T(8,128)(2,1)S(1)} %get-tuple-element.147.hid_ref, bf16[128,7168]{1,0:T(8,128)(2,1)} %get-tuple-element.148.x_ref, f32[128,2]{1,0:T(8,128)S(1)} %get-tuple-element.149.gate_ref, s32[1,512]{1,0:T(1,128)} %bitcast.55, s32[256,1]{1,0:T(8,128)} %add.191.keycol_ref, ...), custom_call_target="tpu_custom_call" | custom-call | tf_op jit(solution)/shard_map/cond/branch_1_fun/down64/pallas_call | solution.py:363
  149.9 1.2 copy.54
  (21 shorter events, 0.2 us)
Async XLA Ops:
  0.0 20.5 %copy-start = (bf16[128,7168]{1,0:T(8,128)(2,1)S(1)}, bf16[128,7168]{1,0:T(8,128)(2,1)}, u32[]{:S(2)}) copy-start(bf16[128,7168]{1,0:T(8,128)(2,1)} %x_ref.1) | copy-start | bytes 5505028
  0.0 19.6 %copy-start.6 = (s32[4]{0:T(128)}, s32[4]{0:T(128)S(1)}, u32[]{:S(2)}) copy-start(s32[4]{0:T(128)S(1)} %iota_multiply_fusion.2) | copy-start | bytes 52
  18.4 0.6 copy-start.1
  76.5 1.3 copy-start.2
  76.5 1.3 copy-start.3
  76.5 1.3 copy-start.4
  76.5 1.3 copy-start.7
  77.9 2.1 %copy-start.8 = (s32[4]{0:T(128)}, s32[4]{0:T(128)S(1)}, u32[]{:S(2)}) copy-start(s32[4]{0:T(128)S(1)} %get-tuple-element.162) | copy-start | bytes 52 | tf_op jit(solution)/shard_map/cond

commit v2 on v1

--- a/solution.py
+++ b/solution.py
@@ -15,8 +15,11 @@
 GROUPS = 4
 UP_STEPS = 14
 UP_BUFS = 4
-DOWN_STEPS = 7
-DOWN_BUFS = 3
+UP_LAG = 3
+DOWN_STEPS = 14
+DOWN_BUFS = 6
+DOWN_LAG = 2
+TIERS = ((64, 176), (128, 256))
 VMEM_LIMIT = 62 * 1024 * 1024
 
 
@@ -29,9 +32,15 @@
     return dp, tp, ep, ep // 2, ep % 2
 
 
-def up_kernel(x_ref, g_ref, wr_hbm, wg_hbm, wu_hbm, tok_ref, choice_ref, hid_ref, gate_ref,
-              u_ref, xs_ref, pick_ref, acc_ref, wbuf, wr_ref, logit_ref,
-              w_sem, wr_sem, own_s, own_r, x_s, x_r, y_s, y_r, dx_s, dx_r, dy_s, dy_r):
+def column(row):
+    n = row.shape[1]
+    eye = lax.broadcasted_iota(jnp.int32, (n, n), 0) == lax.broadcasted_iota(jnp.int32, (n, n), 1)
+    return jnp.sum(jnp.where(eye, row.astype(F32), 0.0), axis=1, keepdims=True).astype(jnp.int32)
+
+
+def up_kernel(x_ref, g_ref, wr_hbm, wg_hbm, wu_hbm, choice_ref, hid_ref, gate_ref, tab_ref, flag_ref,
+              u_ref, xs_ref, pick_ref, acc_ref, wbuf, wr_ref, logit_ref, ch_ref,
+              w_sem, wr_sem, c_s, c_r, own_s, own_r, x_s, x_r, y_s, y_r, dx_s, dx_r, dy_s, dy_r):
     dp, tp, ep, cx, core = place()
     local = wg_hbm.shape[0]
     tok, d_model = x_ref.shape
@@ -40,11 +49,12 @@
     cw = half // steps
     twin = (dp, tp, cx * 2 + (1 - core))
     across = (dp, tp, (1 - cx) * 2 + core)
+    far_twin = (dp, tp, (1 - cx) * 2 + (1 - core))
     other_tp = (dp, 1 - tp, ep)
     far = (1 - cx) * 2 + core
 
     barrier = pltpu.get_barrier_semaphore()
-    for peer in (twin, across, other_tp):
+    for peer in (twin, across, far_twin, other_tp):
         pl.semaphore_signal(barrier, inc=1, device_id=peer, device_id_type=MESH)
 
     def weight_copies(step, slot):
@@ -63,23 +73,28 @@
         for c in weight_copies(b, b):
             c.start()
 
+    scale = g_ref[...].astype(F32).reshape(1, d_model)
+
     def norm_rows(r, carry):
         rows = pl.ds(pl.multiple_of(r * 16, 16), 16)
         xb = x_ref[rows, :].astype(F32)
         cen = xb - jnp.mean(xb, axis=-1, keepdims=True)
         var = jnp.mean(cen * cen, axis=-1, keepdims=True)
-        u = (cen * lax.rsqrt(var + NORM_EPS) * g_ref[...].astype(F32)).astype(BF16)
+        u = (cen * lax.rsqrt(var + NORM_EPS) * scale).astype(BF16)
         for j in range(steps):
             for h in range(2):
                 u_ref[j, h, ep, rows, :] = u[:, h * half + j * cw:h * half + (j + 1) * cw]
         return carry
 
     lax.fori_loop(0, tok // 16, norm_rows, 0)
-    slots = tok_ref.shape[0]
-    pick_ref[...] = jnp.where(tok_ref[...] == lax.broadcasted_iota(jnp.int32, (slots, GROUPS * tok), 1), 1.0, 0.0).astype(BF16)
-    acc_ref[...] = jnp.zeros_like(acc_ref)
-    logit_ref[...] = jnp.zeros_like(logit_ref)
-    pl.semaphore_wait(barrier, 3)
+    pl.semaphore_wait(barrier, 4)
+
+    def choice_copy(n):
+        peer = (across, far_twin, twin)[n]
+        return remote(choice_ref, ch_ref.at[ep], c_s.at[n], c_r.at[n], peer)
+
+    for n in range(3):
+        choice_copy(n).start()
 
     def own_copy(j):
         return remote(u_ref.at[j, :, ep], u_ref.at[j, :, ep], own_s.at[j], own_r.at[j], twin)
@@ -102,7 +117,48 @@
         return carry
 
     lax.fori_loop(0, steps, first_sends, 0)
+    ch_ref[ep] = choice_ref[...]
+    acc_ref[...] = jnp.zeros_like(acc_ref)
+    logit_ref[...] = jnp.zeros_like(logit_ref)
     wr_copy.wait()
+    for n in range(3):
+        choice_copy(n).wait_recv()
+
+    slots = pick_ref.shape[0]
+    upper = jnp.where(lax.broadcasted_iota(jnp.int32, (tok, tok), 0) < lax.broadcasted_iota(jnp.int32, (tok, tok), 1), 1.0, 0.0).astype(BF16)
+    ids = lax.broadcasted_iota(jnp.int32, (tok, tok), 0)
+    lane16 = lax.broadcasted_iota(jnp.int32, (16, tok), 0)
+    slot_iota = lax.broadcasted_iota(jnp.int32, (slots, tok), 0)
+    most = jnp.zeros((16, 1), F32)
+    for g in range(GROUPS):
+        c = [ch_ref[g, j:j + 1, :] for j in range(2)]
+        hot = [jnp.where(ids == c[j], 1.0, 0.0) for j in range(2)]
+        earlier = jnp.dot((hot[0] + hot[1]).astype(BF16), upper, preferred_element_type=F32)
+        pos = [jnp.sum(earlier * hot[j], axis=0, keepdims=True).astype(jnp.int32) for j in range(2)]
+        kept = [pos[j] < CAP for j in range(2)]
+        keptf = [jnp.where(kept[j], 1.0, 0.0) for j in range(2)]
+        owner = [c[j] // 32 for j in range(2)]
+        mine = [jnp.where(lane16 == owner[j], keptf[j], 0.0) for j in range(2)]
+        every = [jnp.where(lane16 == GROUPS, keptf[j], 0.0) for j in range(2)]
+        tally = mine[0] + mine[1] + every[0] + every[1]
+        before = jnp.dot(tally.astype(BF16), upper, preferred_element_type=F32)
+        most = jnp.maximum(most, jnp.sum(tally, axis=1, keepdims=True))
+        rank = [jnp.sum(before * mine[j], axis=0, keepdims=True) for j in range(2)]
+        rank[1] = rank[1] + jnp.where(owner[0] == owner[1], keptf[0], 0.0)
+        nrank = [before[GROUPS:GROUPS + 1, :], before[GROUPS:GROUPS + 1, :] + keptf[0]]
+        for j in range(2):
+            slot = jnp.where(kept[j] & (owner[j] == ep), (c[j] - ep * 32) * 16 + g * CAP + pos[j], -1)
+            tab_ref[g, j:j + 1, :] = slot
+            tab_ref[g, 2 + j:3 + j, :] = jnp.where(kept[j], owner[j] * 128 + rank[j].astype(jnp.int32), -1)
+            tab_ref[g, 4 + j:5 + j, :] = jnp.where(kept[j], nrank[j].astype(jnp.int32), -1)
+        tab_ref[g, 6:8, :] = jnp.zeros((2, tok), jnp.int32)
+        pick_ref[:, g * tok:(g + 1) * tok] = jnp.where((slot_iota == tab_ref[g, 0:1, :]) | (slot_iota == tab_ref[g, 1:2, :]), 1.0, 0.0).astype(BF16)
+    sub16 = lax.broadcasted_iota(jnp.int32, (16, 1), 0)
+    fits = [jnp.where(sub16 < GROUPS, rows_c, jnp.where(sub16 == GROUPS, rows_n, 0)).astype(F32) for rows_c, rows_n in TIERS[:-1]]
+    level = jnp.zeros((1, 1), F32)
+    for f in fits:
+        level = level + jnp.max(jnp.where(most > f, 1.0, 0.0), axis=0, keepdims=True)
+    flag_ref[...] = jnp.broadcast_to(level, flag_ref.shape).astype(jnp.int32)
 
     def main(i, carry):
         @pl.when(i < steps)
@@ -111,15 +167,15 @@
             y_copy(i).start()
             dx_copy(i).start()
 
-        @pl.when((i >= 1) & (i < steps + 1))
-        def _():
-            j = i - 1
+        @pl.when((i >= UP_LAG) & (i < steps + UP_LAG))
+        def _():
+            j = i - UP_LAG
             y_copy(j).wait_recv()
             dy_copy(j).start()
 
-        @pl.when(i >= 2)
-        def _():
-            j = i - 2
+        @pl.when(i >= UP_LAG + 1)
+        def _():
+            j = i - UP_LAG - 1
             slot = lax.rem(j, UP_BUFS)
             for h in range(2):
                 kr = pl.ds(pl.multiple_of(h * half + j * cw, cw), cw)
@@ -148,18 +204,17 @@
                     c.start()
         return carry
 
-    lax.fori_loop(0, steps + 2, main, 0)
+    lax.fori_loop(0, steps + UP_LAG + 1, main, 0)
 
     gate_act = acc_ref[:, :128]
     hid_ref[...] = (gate_act * jax.nn.sigmoid(gate_act) * acc_ref[:, 128:]).astype(BF16)
     logits = logit_ref[...]
     ex = jnp.exp(logits - jnp.max(logits, axis=-1, keepdims=True))
     probs = ex / jnp.sum(ex, axis=-1, keepdims=True)
-    ids = lax.broadcasted_iota(jnp.int32, probs.shape, 1)
-    p0 = jnp.sum(jnp.where(choice_ref[:, 0:1] == ids, probs, 0.0), axis=-1, keepdims=True)
-    p1 = jnp.sum(jnp.where(choice_ref[:, 1:2] == ids, probs, 0.0), axis=-1, keepdims=True)
-    gate_ref[:, 0:1] = p0 / (p0 + p1)
-    gate_ref[:, 1:2] = p1 / (p0 + p1)
+    lanes = lax.broadcasted_iota(jnp.int32, probs.shape, 1)
+    picked = [jnp.sum(jnp.where(column(ch_ref[ep, j:j + 1, :]) == lanes, probs, 0.0), axis=-1, keepdims=True) for j in range(2)]
+    for j in range(2):
+        gate_ref[:, j:j + 1] = picked[j] / (picked[0] + picked[1])
 
     def last_waits(j, carry):
         x_copy(j).wait_send()
@@ -170,9 +225,11 @@
         return carry
 
     lax.fori_loop(0, steps, last_waits, 0)
-
-
-def down_kernel(rows_c, rows_n, hid_ref, x_ref, gate_ref, slotkey_ref, keycol_ref, keyrow_ref, nkey_ref, poskey_ref, npos_ref, wd_hbm, out_ref,
+    for n in range(3):
+        choice_copy(n).wait_send()
+
+
+def down_kernel(rows_c, rows_n, hid_ref, x_ref, gate_ref, tab_ref, wd_hbm, out_ref,
                 send_ref, land_ref, fwd_ref, yland_ref, qs_ref, w2buf, p_ref, s_ref, a_ref, b_ref,
                 w_sem, q_s, q_r, f_s, f_r, o_s, o_r):
     dp, tp, ep, cx, core = place()
@@ -200,18 +257,46 @@
         for c in weight_copies(b, b):
             c.start()
 
-    p_ref[...] = jnp.where(keycol_ref[...] == slotkey_ref[...], 1.0, 0.0).astype(BF16)
-    s_ref[...] = jnp.where(lax.broadcasted_iota(jnp.int32, s_ref.shape, 0) == nkey_ref[...], 1.0, 0.0).astype(BF16)
+    all_rows = GROUPS * rows_c
+    slots = qs_ref.shape[0]
+    gap = 128 - rows_c
+    slot_iota = lax.broadcasted_iota(jnp.int32, (slots, tok), 0)
+    c_iota = lax.broadcasted_iota(jnp.int32, (rows_c, tok), 0)
+
+    def key_of(r):
+        for n in range(1, GROUPS):
+            r = r + jnp.where(r >= n * rows_c + (n - 1) * gap, gap, 0)
+        return r
+
+    def onehot(rows, values):
+        return jnp.where(rows == values, 1.0, 0.0).astype(BF16)
+
+    def times_t(a, b):
+        return lax.dot_general(a, b, (((1,), (1,)), ((), ())), preferred_element_type=F32)
+
+    for g in range(GROUPS):
+        total = jnp.zeros((rows_c, slots), F32)
+        for j in range(2):
+            total += times_t(onehot(c_iota + ep * 128, tab_ref[g, 2 + j:3 + j, :]), onehot(slot_iota, tab_ref[g, j:j + 1, :]))
+        p_ref[g * rows_c:(g + 1) * rows_c, :] = total.astype(BF16)
+    key_iota = key_of(lax.broadcasted_iota(jnp.int32, (all_rows, tok), 0))
+    n_iota = lax.broadcasted_iota(jnp.int32, (rows_n, tok), 0)
+    my_key = [tab_ref[ep, 2 + j:3 + j, :] for j in range(2)]
+    my_n = [tab_ref[ep, 4 + j:5 + j, :] for j in range(2)]
+    total = jnp.zeros((rows_n, all_rows), F32)
+    for j in range(2):
+        total += times_t(onehot(n_iota, my_n[j]), onehot(key_iota, my_key[j]))
+    s_ref[...] = total.astype(BF16)
 
     def split_gates(keys, pos, dst):
-        mat = jnp.where(pos[:, 0:1] == keys, gate_ref[:, 0:1], 0.0) + jnp.where(pos[:, 1:2] == keys, gate_ref[:, 1:2], 0.0)
+        mat = jnp.where(pos[0] == keys, gate_ref[:, 0:1], 0.0) + jnp.where(pos[1] == keys, gate_ref[:, 1:2], 0.0)
         for z in range(3):
             part = mat.astype(BF16)
             dst[z] = part
             mat = mat - part.astype(F32)
 
-    split_gates(keyrow_ref[...], poskey_ref[...], a_ref)
-    split_gates(lax.broadcasted_iota(jnp.int32, (tok, rows_n), 1), npos_ref[...], b_ref)
+    split_gates(key_of(lax.broadcasted_iota(jnp.int32, (tok, all_rows), 1)), [column(v) for v in my_key], a_ref)
+    split_gates(lax.broadcasted_iota(jnp.int32, (tok, rows_n), 1), [column(v) for v in my_n], b_ref)
     pl.semaphore_wait(barrier, 4)
 
     def q_copy(k, n):
@@ -250,18 +335,18 @@
             for n in range(3):
                 q_copy(i, n).start()
 
-        @pl.when((i >= 1) & (i < steps + 1))
-        def _():
-            k = i - 1
+        @pl.when((i >= DOWN_LAG) & (i < steps + DOWN_LAG))
+        def _():
+            k = i - DOWN_LAG
             for n in range(3):
                 q_copy(k, n).wait_recv()
             block = land_ref[k, 1 - tp].reshape(GROUPS * rows_c, cw)
             fwd_ref[k] = jnp.dot(s_ref[...], block, preferred_element_type=F32).astype(BF16)
             f_copy(k).start()
 
-        @pl.when(i >= 2)
-        def _():
-            k = i - 2
+        @pl.when(i >= 2 * DOWN_LAG)
+        def _():
+            k = i - 2 * DOWN_LAG
             mine = land_ref[k, tp].reshape(GROUPS * rows_c, cw)
             mix = jnp.dot(a_ref[2], mine, preferred_element_type=F32)
             mix += jnp.dot(a_ref[1], mine, preferred_element_type=F32)
@@ -275,7 +360,7 @@
             o_copy(k).start()
         return carry
 
-    lax.fori_loop(0, steps + 2, main, 0)
+    lax.fori_loop(0, steps + 2 * DOWN_LAG, main, 0)
 
     def last_waits(k, carry):
         for n in range(3):
@@ -289,52 +374,24 @@
     lax.fori_loop(0, steps, last_waits, 0)
 
 
-def routing(choice):
-    ep = lax.axis_index('ep')
-    pairs = choice.shape[0] * choice.shape[1]
-    ids = lax.all_gather(choice, 'ep', tiled=True).reshape(GROUPS, pairs)
-    onehot = (ids[:, :, None] == jnp.arange(128, dtype=jnp.int32)).astype(BF16)
-    order = jnp.arange(pairs, dtype=jnp.int32)
-    tri = (order[:, None] > order[None, :]).astype(BF16)
-    earlier = jnp.einsum('pq,gqe->gpe', tri, onehot, preferred_element_type=F32)
-    position = jnp.sum(earlier * onehot.astype(F32), axis=-1).astype(jnp.int32)
-    kept = position < CAP
-    owner = ids // 32
-    hot = ((owner[:, :, None] == jnp.arange(GROUPS, dtype=jnp.int32)) & kept[:, :, None])
-    hot = jnp.concatenate([hot, kept[:, :, None]], axis=-1).astype(BF16)
-    before = jnp.einsum('pq,gqe->gpe', tri, hot, preferred_element_type=F32)
-    rank = jnp.sum((before * hot.astype(F32))[:, :, :GROUPS], axis=-1).astype(jnp.int32)
-    nrank = before[:, :, GROUPS].astype(jnp.int32)
-    count = jnp.sum(hot.astype(F32), axis=1).astype(jnp.int32)
-    max_c = jnp.max(count[:, :GROUPS])
-    max_n = jnp.max(count[:, GROUPS])
-    group = jnp.arange(GROUPS, dtype=jnp.int32)[:, None]
-    slot = jnp.where(kept & (owner == ep), (ids - ep * 32) * 16 + group * CAP + position, -1).reshape(-1)
-    token = (group * (pairs // 2) + order[None, :] // 2).reshape(-1)
-    match = slot[None, :] == jnp.arange(512, dtype=jnp.int32)[:, None]
-    tok_of = jnp.max(jnp.where(match, token[None, :], -1), axis=1)
-    slotkey = jnp.max(jnp.where(match, (group * 128 + rank).reshape(-1)[None, :], -1), axis=1)
-    key = jnp.where(kept, owner * 128 + rank, -1)
-    npos = jnp.where(kept, nrank, -1)
-    my_key = lax.dynamic_index_in_dim(key, ep, 0, keepdims=False)
-    my_n = lax.dynamic_index_in_dim(npos, ep, 0, keepdims=False)
-    nkey = jnp.max(jnp.where(my_key[None, :] == jnp.arange(512, dtype=jnp.int32)[:, None], my_n[None, :], -1), axis=1)
-    return tok_of[:, None], slotkey[None, :], my_key.reshape(-1, 2), my_n.reshape(-1, 2), nkey.reshape(GROUPS, 128), max_c, max_n
-
-
-def run_up(x, g, wr, wg, wu, tok_of, choice):
+def run_up(x, g, wr, wg, wu, choice_t):
     tok, d_model = x.shape
     local = wg.shape[0]
     cw = d_model // 2 // UP_STEPS
-    slots = tok_of.shape[0]
+    slots = local * GROUPS * CAP
     vm = pl.BlockSpec(memory_space=pltpu.VMEM)
     hbm = pl.BlockSpec(memory_space=pl.ANY)
     sem = pltpu.SemaphoreType.DMA
     return pl.pallas_call(
         up_kernel,
-        out_shape=(jax.ShapeDtypeStruct((slots, 128), BF16), jax.ShapeDtypeStruct((tok, 2), F32)),
-        in_specs=[vm, vm, hbm, hbm, hbm, vm, vm],
-        out_specs=(vm, vm),
+        out_shape=(
+            jax.ShapeDtypeStruct((slots, 128), BF16),
+            jax.ShapeDtypeStruct((tok, 2), F32),
+            jax.ShapeDtypeStruct((GROUPS, 8, tok), jnp.int32),
+            jax.ShapeDtypeStruct((8, 128), jnp.int32),
+        ),
+        in_specs=[vm, vm, hbm, hbm, hbm, vm],
+        out_specs=(vm, vm, vm, vm),
         scratch_shapes=[
             pltpu.VMEM((UP_STEPS, 2, GROUPS, tok, cw), BF16),
             pltpu.VMEM((slots, 2 * cw), BF16),
@@ -343,27 +400,27 @@
             pltpu.VMEM((UP_BUFS, local, 2 * cw, 256), BF16),
             pltpu.VMEM(wr.shape, BF16),
             pltpu.VMEM((tok, 128), F32),
-            sem((UP_BUFS, 4)), sem,
+            pltpu.VMEM((GROUPS, 2, tok), jnp.int32),
+            sem((UP_BUFS, 4)), sem, sem((3,)), sem((3,)),
         ] + [sem((UP_STEPS,))] * 10,
         compiler_params=pltpu.CompilerParams(collective_id=0, has_side_effects=True, vmem_limit_bytes=VMEM_LIMIT),
         name='up',
-    )(x, g, wr, wg, wu, tok_of, choice)
-
-
-def run_down(tier, rows_c, rows_n, hid, x, gate, slotkey, poskey, npos, nkey, wd):
+    )(x, g, wr, wg, wu, choice_t)
+
+
+def run_down(tier, hid, x, gate, tab, wd):
+    rows_c, rows_n = TIERS[tier]
     tok, d_model = x.shape
     local = wd.shape[0]
     cw = d_model // 2 // DOWN_STEPS
     slots = hid.shape[0]
-    keys = (jnp.arange(GROUPS, dtype=jnp.int32)[:, None] * 128 + jnp.arange(rows_c, dtype=jnp.int32)[None, :]).reshape(-1)
-    nkey = nkey[:, :rows_c].reshape(1, -1)
     vm = pl.BlockSpec(memory_space=pltpu.VMEM)
     hbm = pl.BlockSpec(memory_space=pl.ANY)
     sem = pltpu.SemaphoreType.DMA
     return pl.pallas_call(
         functools.partial(down_kernel, rows_c, rows_n),
         out_shape=jax.ShapeDtypeStruct(x.shape, BF16),
-        in_specs=[vm] * 9 + [hbm],
+        in_specs=[vm] * 4 + [hbm],
         out_specs=vm,
         scratch_shapes=[
             pltpu.VMEM((DOWN_STEPS, 2, GROUPS, rows_c, cw), BF16),
@@ -381,17 +438,14 @@
         ],
         compiler_params=pltpu.CompilerParams(collective_id=1 + tier, has_side_effects=True, vmem_limit_bytes=VMEM_LIMIT),
         name='down%d' % rows_c,
-    )(hid, x, gate, slotkey, keys[:, None], keys[None, :], nkey, poskey, npos, wd)
+    )(hid, x, gate, tab, wd)
 
 
 def solution(mesh):
     row_spec = P(('dp', 'ep'), None)
 
     def device_step(resid_in, norm_scale, w_router, w_gate, w_up, w_down, choice):
-        tok_of, slotkey, poskey, npos, nkey, max_c, max_n = routing(choice)
-        hid, gate = run_up(resid_in, norm_scale[None, :], w_router, w_gate, w_up, tok_of, choice)
-        args = (hid, resid_in, gate, slotkey, poskey, npos, nkey, w_down)
-        small = (max_c <= 64) & (max_n <= 176)
-        return lax.cond(small, functools.partial(run_down, 0, 64, 176), functools.partial(run_down, 1, 128, 256), *args)
+        hid, gate, tab, flag = run_up(resid_in, norm_scale, w_router, w_gate, w_up, choice.T)
+        return lax.switch(flag[0, 0], [functools.partial(run_down, t) for t in range(len(TIERS))], hid, resid_in, gate, tab, w_down)
 
     return jax.shard_map(device_step, mesh=mesh, in_specs=(row_spec, P(None), P(None, None), P('ep', None, 'tp'), P('ep', None, 'tp'), P('ep', 'tp', None), row_spec), out_specs=row_spec, check_vma=False)

time: 151 us -> 124 us (0.82)
  blocking collectives: 9.94 us -> 0 us
  other arithmetic: 8.23 us -> 0 us
  local copies, waits for them, and re-layouts: 10.5 us -> 4.04 us
    all_gather x1 -> x0, blocking collectives: 9.94 us -> none  [routing(): ids = lax.all_gather(choice, 'ep', tiled=True).reshape(GROUPS, pairs)]
    reduce_max x5 -> x0, other arithmetic: 3.51 us -> none  [the longest x1 1.03 us: routing(): tok_of = jnp.max(jnp.where(match, token[None, :], -1), axis=1)]
    reshape x5 -> x0, local copies, waits for them, and re-layouts: 2.5 us -> none  [the longest x1 0.76 us: routing(): my_key.reshape(-1, 2)]
    broadcast_in_dim x3 -> x0, local copies, waits for them, and re-layouts: 2.43 us -> none  [the longest x1 1.33 us: device_step(): norm_scale[None, :]]
    cond x3 -> x0, other arithmetic: 2.14 us -> none
    pallas_call x1, Pallas kernels: 64.4 us -> 62.8 us  [run_down(): pl.pallas_call(functools.partial(down_kernel, rows_c, rows_n), out_shape=...]
    unnamed x21 -> x3, local copies, waits for them, and re-layouts: 3.33 us -> 2.85 us
where the time goes in v2:
time: 124 us
  Pallas kernels  119 us (96%)
  local copies, waits for them, and re-layouts  4.04 us (3%)
    pallas_call x1, Pallas kernels, run_down(): pl.pallas_call(functools.partial(down_kernel, rows_c, rows_n), out_shape=...  62.8 us
    pallas_call x1, Pallas kernels, run_up(): pl.pallas_call(up_kernel, out_shape=(jax.ShapeDtypeStruct((slots, 128), B...  56.3 us
    unnamed x3, local copies, waits for them, and re-layouts  2.85 us

profile of v2, /device:TPU:0, one launch (start us, length us, event | category | flops | bytes accessed | tf_op | source)
XLA Modules:
  0.0 123.8 jit_solution(18442082587463230251)
XLA Ops:
  0.0 0.0 copy-start
  0.0 56.3 %up.1 = (bf16[512,128]{1,0:T(8,128)(2,1)S(1)}, f32[128,2]{1,0:T(8,128)S(1)}, s32[4,8,128]{2,1,0:T(8,128)}, s32[8,128]{1,0:T(8,128)}) custom-call(bf16[128,7168]{1,0:T(8,128)(2,1)} %x_ref.1, bf16[7168]{0:T(1024)(128)(2,1)} %g_ref.1, bf16[7168,128]{1,0:T(8,128)(2,1)} %wr_hbm.1, bf16[32,7168,128]{2,1,0:T(8,128)(2,1)} %wg_hbm.1, bf16[32,7168,128]{2,1,0:T(8,128)(2,1)} %wu_hbm.1, ...), custom_call_target="tpu_custom_call" | custom-call | tf_op jit(solution)/shard_map/up/pallas_call | solution.py:385
  56.3 1.2 slice.3
  58.1 0.0 copy-done
  58.1 62.8 %conditional.1 = (bf16[128,7168]{1,0:T(8,128)(2,1)}) conditional(s32[]{:T(128)} %bitcast.1, (bf16[512,128]{1,0:T(8,128)(2,1)S(1)}, bf16[128,7168]{1,0:T(8,128)(2,1)S(1)}, f32[128,2]{1,0:T(8,128)S(1)}, s32[4,8,128]{2,1,0:T(8,128)}, bf16[32,128,7168]{2,1,0:T(8,128)(2,1)}) %tuple.16, (bf16[512,128]{1,0:T(8,128)(2,1)S(1)}, ...), branch_computations={%region_0.0_spmd, %region_1.0_spmd} | conditional | bytes 8 | solution.py:449
  58.2 62.8 %down64.1 = bf16[128,7168]{1,0:T(8,128)(2,1)} custom-call(bf16[512,128]{1,0:T(8,128)(2,1)S(1)} %get-tuple-element.28.hid_ref, bf16[128,7168]{1,0:T(8,128)(2,1)S(1)} %get-tuple-element.29.x_ref, f32[128,2]{1,0:T(8,128)S(1)} %get-tuple-element.30.gate_ref, s32[4,8,128]{2,1,0:T(8,128)} %get-tuple-element.31.tab_ref, bf16[32,128,7168]{2,1,0:T(8,128)(2,1)} %get-tuple-element.49.wd_hbm), custom_call_target="tpu_custom_call" | custom-call | tf_op jit(solution)/shard_map/cond/branch_0_fun/down64/pallas_call | solution.py:420
  121.0 2.8 %copy.15 = bf16[128,7168]{1,0:T(8,128)(2,1)} copy(bf16[128,7168]{1,0:T(8,128)(2,1)} %get-tuple-element.46) | data formatting | bytes 3670016
Async XLA Ops:
  0.0 58.1 %copy-start = (bf16[128,7168]{1,0:T(8,128)(2,1)S(1)}, bf16[128,7168]{1,0:T(8,128)(2,1)}, u32[]{:S(2)}) copy-start(bf16[128,7168]{1,0:T(8,128)(2,1)} %x_ref.1) | copy-start | bytes 5505028

commit v3 on v2

--- a/solution.py
+++ b/solution.py
@@ -20,7 +20,8 @@
 DOWN_BUFS = 6
 DOWN_LAG = 2
 TIERS = ((64, 176), (128, 256))
-VMEM_LIMIT = 62 * 1024 * 1024
+DOWN_VMEM = (46 * 1024 * 1024, 56 * 1024 * 1024)
+VMEM_LIMIT = 58 * 1024 * 1024
 
 
 def remote(src, dst, send_sem, recv_sem, device):
@@ -62,7 +63,7 @@
         for h in range(2):
             rows = pl.ds(pl.multiple_of(h * half + step * cw, cw), cw)
             for m, w in enumerate((wg_hbm, wu_hbm)):
-                out.append(pltpu.make_async_copy(w.at[:, rows, :], wbuf.at[slot, :, h * cw:(h + 1) * cw, m * 128:(m + 1) * 128], w_sem.at[slot, h * 2 + m]))
+                out.append(pltpu.make_async_copy(w.at[:, rows, :], wbuf.at[slot, m, :, h * cw:(h + 1) * cw, :], w_sem.at[slot, h * 2 + m]))
         return out
 
     wr_copy = pltpu.make_async_copy(wr_hbm, wr_ref, wr_sem)
@@ -158,7 +159,7 @@
     level = jnp.zeros((1, 1), F32)
     for f in fits:
         level = level + jnp.max(jnp.where(most > f, 1.0, 0.0), axis=0, keepdims=True)
-    flag_ref[...] = jnp.broadcast_to(level, flag_ref.shape).astype(jnp.int32)
+    flag_ref[0] = jnp.max(level).astype(jnp.int32)
 
     def main(i, carry):
         @pl.when(i < steps)
@@ -193,7 +194,7 @@
                 for z in range(4):
                     e = t * 4 + z
                     rows = pl.ds(pl.multiple_of(e * 16, 16), 16)
-                    acc_ref[rows, :] += jnp.dot(xs_ref[rows, :], wbuf[slot, e], preferred_element_type=F32)
+                    acc_ref[rows, :] += jnp.dot(xs_ref[rows, :], jnp.concatenate([wbuf[slot, 0, e], wbuf[slot, 1, e]], axis=1), preferred_element_type=F32)
                 return carry2
 
             lax.fori_loop(0, local // 4, experts, 0)
@@ -388,16 +389,16 @@
             jax.ShapeDtypeStruct((slots, 128), BF16),
             jax.ShapeDtypeStruct((tok, 2), F32),
             jax.ShapeDtypeStruct((GROUPS, 8, tok), jnp.int32),
-            jax.ShapeDtypeStruct((8, 128), jnp.int32),
+            jax.ShapeDtypeStruct((1,), jnp.int32),
         ),
         in_specs=[vm, vm, hbm, hbm, hbm, vm],
-        out_specs=(vm, vm, vm, vm),
+        out_specs=(vm, vm, vm, pl.BlockSpec(memory_space=pltpu.SMEM)),
         scratch_shapes=[
             pltpu.VMEM((UP_STEPS, 2, GROUPS, tok, cw), BF16),
             pltpu.VMEM((slots, 2 * cw), BF16),
             pltpu.VMEM((slots, GROUPS * tok), BF16),
             pltpu.VMEM((slots, 256), F32),
-            pltpu.VMEM((UP_BUFS, local, 2 * cw, 256), BF16),
+            pltpu.VMEM((UP_BUFS, 2, local, 2 * cw, 128), BF16),
             pltpu.VMEM(wr.shape, BF16),
             pltpu.VMEM((tok, 128), F32),
             pltpu.VMEM((GROUPS, 2, tok), jnp.int32),
@@ -436,7 +437,7 @@
             sem((DOWN_BUFS, 2)), sem((DOWN_STEPS, 3)), sem((DOWN_STEPS, 3)),
             sem((DOWN_STEPS,)), sem((DOWN_STEPS,)), sem((DOWN_STEPS,)), sem((DOWN_STEPS,)),
         ],
-        compiler_params=pltpu.CompilerParams(collective_id=1 + tier, has_side_effects=True, vmem_limit_bytes=VMEM_LIMIT),
+        compiler_params=pltpu.CompilerParams(collective_id=1 + tier, has_side_effects=True, vmem_limit_bytes=DOWN_VMEM[tier]),
         name='down%d' % rows_c,
     )(hid, x, gate, tab, wd)
 
@@ -446,6 +447,6 @@
 
     def device_step(resid_in, norm_scale, w_router, w_gate, w_up, w_down, choice):
         hid, gate, tab, flag = run_up(resid_in, norm_scale, w_router, w_gate, w_up, choice.T)
-        return lax.switch(flag[0, 0], [functools.partial(run_down, t) for t in range(len(TIERS))], hid, resid_in, gate, tab, w_down)
+        return lax.switch(flag[0], [functools.partial(run_down, t) for t in range(len(TIERS))], hid, resid_in, gate, tab, w_down)
 
     return jax.shard_map(device_step, mesh=mesh, in_specs=(row_spec, P(None), P(None, None), P('ep', None, 'tp'), P('ep', None, 'tp'), P('ep', 'tp', None), row_spec), out_specs=row_spec, check_vma=False)

time: 124 us -> 123 us (level)
  local copies, waits for them, and re-layouts: 4.04 us -> 1.23 us
  Pallas kernels: 119 us -> 121 us
    pallas_call x1, Pallas kernels: 56.3 us -> 60.4 us  [run_up(): pl.pallas_call(up_kernel, out_shape=(jax.ShapeDtypeStruct((slots, 128), B...]
    pallas_call x1, Pallas kernels: 62.8 us -> 60.6 us  [run_down(): pl.pallas_call(functools.partial(down_kernel, rows_c, rows_n), out_shape=...]
    unnamed x3, local copies, waits for them, and re-layouts: 2.85 us -> 1.23 us
where the time goes in v3:
time: 123 us
  Pallas kernels  121 us (98%)
  local copies, waits for them, and re-layouts  1.23 us (1%)
    pallas_call x1, Pallas kernels, run_down(): pl.pallas_call(functools.partial(down_kernel, rows_c, rows_n), out_shape=...  60.6 us
    pallas_call x1, Pallas kernels, run_up(): pl.pallas_call(up_kernel, out_shape=(jax.ShapeDtypeStruct((slots, 128), B...  60.4 us

profile of v3, /device:TPU:0, one launch (start us, length us, event | category | flops | bytes accessed | tf_op | source)
XLA Modules:
  0.0 123.0 jit_solution(16490467807073546938)
XLA Ops:
  0.0 0.0 copy-start
  0.0 60.4 %up.1 = (bf16[512,128]{1,0:T(8,128)(2,1)S(1)}, f32[128,2]{1,0:T(8,128)S(1)}, s32[4,8,128]{2,1,0:T(8,128)S(1)}, s32[1]{0:T(128)}) custom-call(bf16[128,7168]{1,0:T(8,128)(2,1)} %x_ref.1, bf16[7168]{0:T(1024)(128)(2,1)} %g_ref.1, bf16[7168,128]{1,0:T(8,128)(2,1)} %wr_hbm.1, bf16[32,7168,128]{2,1,0:T(8,128)(2,1)} %wg_hbm.1, bf16[32,7168,128]{2,1,0:T(8,128)(2,1)} %wu_hbm.1, ...), custom_call_target="tpu_custom_call" | custom-call | tf_op jit(solution)/shard_map/up/pallas_call | solution.py:386
  61.1 0.0 copy-done
  61.1 60.7 %conditional.1 = (bf16[128,7168]{1,0:T(8,128)(2,1)S(1)}) conditional(s32[]{:T(128)} %bitcast.1, (bf16[512,128]{1,0:T(8,128)(2,1)S(1)}, bf16[128,7168]{1,0:T(8,128)(2,1)S(1)}, f32[128,2]{1,0:T(8,128)S(1)}, s32[4,8,128]{2,1,0:T(8,128)S(1)}, bf16[32,128,7168]{2,1,0:T(8,128)(2,1)}) %tuple.16, (bf16[512,128]{1,0:T(8,128)(2,1)S(1)}, ...), branch_computations={%region_0.0_spmd, %region_1.0_spmd} | conditional | bytes 8 | solution.py:450
  61.1 60.6 %down64.1 = bf16[128,7168]{1,0:T(8,128)(2,1)S(1)} custom-call(bf16[512,128]{1,0:T(8,128)(2,1)S(1)} %get-tuple-element.28.hid_ref, bf16[128,7168]{1,0:T(8,128)(2,1)S(1)} %get-tuple-element.29.x_ref, f32[128,2]{1,0:T(8,128)S(1)} %get-tuple-element.30.gate_ref, s32[4,8,128]{2,1,0:T(8,128)S(1)} %get-tuple-element.31.tab_ref, ...), custom_call_target="tpu_custom_call" | custom-call | tf_op jit(solution)/shard_map/cond/branch_0_fun/down64/pallas_call | solution.py:421
  121.7 1.2 %copy.15 = bf16[128,7168]{1,0:T(8,128)(2,1)} copy(bf16[128,7168]{1,0:T(8,128)(2,1)S(1)} %get-tuple-element.46) | data formatting | bytes 3670016
Async XLA Ops:
  0.0 61.1 %copy-start = (bf16[128,7168]{1,0:T(8,128)(2,1)S(1)}, bf16[128,7168]{1,0:T(8,128)(2,1)}, u32[]{:S(2)}) copy-start(bf16[128,7168]{1,0:T(8,128)(2,1)} %x_ref.1) | copy-start | bytes 5505028

commit v4 on v3

--- a/solution.py
+++ b/solution.py
@@ -14,14 +14,16 @@
 CAP = 4
 GROUPS = 4
 UP_STEPS = 14
-UP_BUFS = 4
+UP_BUFS = 6
+EARLY = 18
+LATE_BUFS = 6
 UP_LAG = 3
 DOWN_STEPS = 14
 DOWN_BUFS = 6
 DOWN_LAG = 2
 TIERS = ((64, 176), (128, 256))
 DOWN_VMEM = (46 * 1024 * 1024, 56 * 1024 * 1024)
-VMEM_LIMIT = 58 * 1024 * 1024
+VMEM_LIMIT = 48 * 1024 * 1024
 
 
 def remote(src, dst, send_sem, recv_sem, device):
@@ -39,11 +41,10 @@
     return jnp.sum(jnp.where(eye, row.astype(F32), 0.0), axis=1, keepdims=True).astype(jnp.int32)
 
 
-def up_kernel(x_ref, g_ref, wr_hbm, wg_hbm, wu_hbm, choice_ref, hid_ref, gate_ref, tab_ref, flag_ref,
-              u_ref, xs_ref, pick_ref, acc_ref, wbuf, wr_ref, logit_ref, ch_ref,
-              w_sem, wr_sem, c_s, c_r, own_s, own_r, x_s, x_r, y_s, y_r, dx_s, dx_r, dy_s, dy_r):
+def up_kernel(x_ref, g_ref, wr_ref, wg_hbm, wu_hbm, choice_ref, hid_ref, late_ref, gate_ref, tab_ref, act_ref, flag_ref,
+              u_ref, xs_ref, pick_ref, acc_ref, wbuf, logit_ref, ch_ref,
+              w_sem, c_s, c_r, own_s, own_r, x_s, x_r, y_s, y_r, dx_s, dx_r, dy_s, dy_r):
     dp, tp, ep, cx, core = place()
-    local = wg_hbm.shape[0]
     tok, d_model = x_ref.shape
     half = d_model // 2
     steps = UP_STEPS
@@ -63,14 +64,10 @@
         for h in range(2):
             rows = pl.ds(pl.multiple_of(h * half + step * cw, cw), cw)
             for m, w in enumerate((wg_hbm, wu_hbm)):
-                out.append(pltpu.make_async_copy(w.at[:, rows, :], wbuf.at[slot, m, :, h * cw:(h + 1) * cw, :], w_sem.at[slot, h * 2 + m]))
+                out.append(pltpu.make_async_copy(w.at[0:EARLY, rows, :], wbuf.at[slot, :, h * cw:(h + 1) * cw, m * 128:(m + 1) * 128], w_sem.at[slot, h * 2 + m]))
         return out
 
-    wr_copy = pltpu.make_async_copy(wr_hbm, wr_ref, wr_sem)
-    for c in weight_copies(0, 0):
-        c.start()
-    wr_copy.start()
-    for b in range(1, UP_BUFS):
+    for b in range(UP_BUFS):
         for c in weight_copies(b, b):
             c.start()
 
@@ -121,7 +118,6 @@
     ch_ref[ep] = choice_ref[...]
     acc_ref[...] = jnp.zeros_like(acc_ref)
     logit_ref[...] = jnp.zeros_like(logit_ref)
-    wr_copy.wait()
     for n in range(3):
         choice_copy(n).wait_recv()
 
@@ -131,6 +127,7 @@
     lane16 = lax.broadcasted_iota(jnp.int32, (16, tok), 0)
     slot_iota = lax.broadcasted_iota(jnp.int32, (slots, tok), 0)
     most = jnp.zeros((16, 1), F32)
+    load = jnp.zeros((tok, 1), F32)
     for g in range(GROUPS):
         c = [ch_ref[g, j:j + 1, :] for j in range(2)]
         hot = [jnp.where(ids == c[j], 1.0, 0.0) for j in range(2)]
@@ -143,6 +140,7 @@
         every = [jnp.where(lane16 == GROUPS, keptf[j], 0.0) for j in range(2)]
         tally = mine[0] + mine[1] + every[0] + every[1]
         before = jnp.dot(tally.astype(BF16), upper, preferred_element_type=F32)
+        load = load + jnp.sum(hot[0] + hot[1], axis=1, keepdims=True)
         most = jnp.maximum(most, jnp.sum(tally, axis=1, keepdims=True))
         rank = [jnp.sum(before * mine[j], axis=0, keepdims=True) for j in range(2)]
         rank[1] = rank[1] + jnp.where(owner[0] == owner[1], keptf[0], 0.0)
@@ -159,6 +157,8 @@
     level = jnp.zeros((1, 1), F32)
     for f in fits:
         level = level + jnp.max(jnp.where(most > f, 1.0, 0.0), axis=0, keepdims=True)
+    diag = ids == lax.broadcasted_iota(jnp.int32, (tok, tok), 1)
+    act_ref[...] = jnp.sum(jnp.where(diag, load, 0.0), axis=0, keepdims=True).astype(jnp.int32)
     flag_ref[0] = jnp.max(level).astype(jnp.int32)
 
     def main(i, carry):
@@ -186,18 +186,20 @@
             dy_copy(j).wait_recv()
             for h in range(2):
                 block = u_ref[j, h].reshape(GROUPS * tok, cw)
-                xs_ref[:, h * cw:(h + 1) * cw] = jnp.dot(pick_ref[...], block, preferred_element_type=F32).astype(BF16)
+                rows_u = jnp.dot(pick_ref[...], block, preferred_element_type=F32).astype(BF16)
+                xs_ref[:, h * cw:(h + 1) * cw] = rows_u[0:EARLY * 16]
+                late_ref[:, pl.ds(pl.multiple_of(h * half + j * cw, cw), cw)] = rows_u[EARLY * 16:]
             for c in weight_copies(j, slot):
                 c.wait()
 
             def experts(t, carry2):
-                for z in range(4):
-                    e = t * 4 + z
+                for z in range(3):
+                    e = t * 3 + z
                     rows = pl.ds(pl.multiple_of(e * 16, 16), 16)
-                    acc_ref[rows, :] += jnp.dot(xs_ref[rows, :], jnp.concatenate([wbuf[slot, 0, e], wbuf[slot, 1, e]], axis=1), preferred_element_type=F32)
+                    acc_ref[rows, :] += jnp.dot(xs_ref[rows, :], wbuf[slot, e], preferred_element_type=F32)
                 return carry2
 
-            lax.fori_loop(0, local // 4, experts, 0)
+            lax.fori_loop(0, EARLY // 3, experts, 0)
 
             @pl.when(j + UP_BUFS < steps)
             def _():
@@ -230,8 +232,50 @@
         choice_copy(n).wait_send()
 
 
-def down_kernel(rows_c, rows_n, hid_ref, x_ref, gate_ref, tab_ref, wd_hbm, out_ref,
-                send_ref, land_ref, fwd_ref, yland_ref, qs_ref, w2buf, p_ref, s_ref, a_ref, b_ref,
+def late_kernel(act_ref, late_ref, wg_hbm, wu_hbm, hid_ref, list_ref, wbuf, w_sem):
+    ep = lax.axis_index('ep')
+    local = wg_hbm.shape[0]
+    hid_ref[...] = jnp.zeros_like(hid_ref)
+
+    def scan(e, n):
+        busy = act_ref[0, ep * local + e] > 0
+
+        @pl.when(busy)
+        def _():
+            list_ref[n] = e
+        return n + busy.astype(jnp.int32)
+
+    count = lax.fori_loop(EARLY, local, scan, 0)
+
+    def weight_copies(n):
+        slot = lax.rem(n, LATE_BUFS)
+        e = list_ref[n]
+        return [pltpu.make_async_copy(w.at[e], wbuf.at[slot, :, m * 128:(m + 1) * 128], w_sem.at[slot, m]) for m, w in enumerate((wg_hbm, wu_hbm))]
+
+    def start(n):
+        @pl.when(n < count)
+        def _():
+            for c in weight_copies(n):
+                c.start()
+
+    for n in range(LATE_BUFS):
+        start(n)
+
+    def step(n, carry):
+        for c in weight_copies(n):
+            c.wait()
+        rows = pl.ds(pl.multiple_of((list_ref[n] - EARLY) * 16, 16), 16)
+        both = jnp.dot(late_ref[rows, :], wbuf[lax.rem(n, LATE_BUFS)], preferred_element_type=F32)
+        gate_act = both[:, :128]
+        hid_ref[rows, :] = (gate_act * jax.nn.sigmoid(gate_act) * both[:, 128:]).astype(BF16)
+        start(n + LATE_BUFS)
+        return carry
+
+    lax.fori_loop(0, count, step, 0)
+
+
+def down_kernel(rows_c, rows_n, early_ref, late_ref, x_ref, gate_ref, tab_ref, wd_hbm, out_ref,
+                hid_ref, send_ref, land_ref, fwd_ref, yland_ref, qs_ref, w2buf, p_ref, s_ref, a_ref, b_ref,
                 w_sem, q_s, q_r, f_s, f_r, o_s, o_r):
     dp, tp, ep, cx, core = place()
     local = wd_hbm.shape[0]
@@ -258,6 +302,8 @@
         for c in weight_copies(b, b):
             c.start()
 
+    hid_ref[0:EARLY * 16, :] = early_ref[...]
+    hid_ref[EARLY * 16:, :] = late_ref[...]
     all_rows = GROUPS * rows_c
     slots = qs_ref.shape[0]
     gap = 128 - rows_c
@@ -381,49 +427,70 @@
     cw = d_model // 2 // UP_STEPS
     slots = local * GROUPS * CAP
     vm = pl.BlockSpec(memory_space=pltpu.VMEM)
-    hbm = pl.BlockSpec(memory_space=pl.ANY)
+    hbm = pl.BlockSpec(memory_space=pltpu.HBM)
     sem = pltpu.SemaphoreType.DMA
     return pl.pallas_call(
         up_kernel,
         out_shape=(
-            jax.ShapeDtypeStruct((slots, 128), BF16),
+            jax.ShapeDtypeStruct((EARLY * 16, 128), BF16),
+            jax.ShapeDtypeStruct((slots - EARLY * 16, d_model), BF16),
             jax.ShapeDtypeStruct((tok, 2), F32),
             jax.ShapeDtypeStruct((GROUPS, 8, tok), jnp.int32),
+            jax.ShapeDtypeStruct((1, 128), jnp.int32),
             jax.ShapeDtypeStruct((1,), jnp.int32),
         ),
-        in_specs=[vm, vm, hbm, hbm, hbm, vm],
-        out_specs=(vm, vm, vm, pl.BlockSpec(memory_space=pltpu.SMEM)),
+        in_specs=[vm, vm, vm, hbm, hbm, vm],
+        out_specs=(vm, vm, vm, vm, vm, pl.BlockSpec(memory_space=pltpu.SMEM)),
         scratch_shapes=[
             pltpu.VMEM((UP_STEPS, 2, GROUPS, tok, cw), BF16),
-            pltpu.VMEM((slots, 2 * cw), BF16),
+            pltpu.VMEM((EARLY * 16, 2 * cw), BF16),
             pltpu.VMEM((slots, GROUPS * tok), BF16),
-            pltpu.VMEM((slots, 256), F32),
-            pltpu.VMEM((UP_BUFS, 2, local, 2 * cw, 128), BF16),
-            pltpu.VMEM(wr.shape, BF16),
+            pltpu.VMEM((EARLY * 16, 256), F32),
+            pltpu.VMEM((UP_BUFS, EARLY, 2 * cw, 256), BF16),
             pltpu.VMEM((tok, 128), F32),
             pltpu.VMEM((GROUPS, 2, tok), jnp.int32),
-            sem((UP_BUFS, 4)), sem, sem((3,)), sem((3,)),
+            sem((UP_BUFS, 4)), sem((3,)), sem((3,)),
         ] + [sem((UP_STEPS,))] * 10,
         compiler_params=pltpu.CompilerParams(collective_id=0, has_side_effects=True, vmem_limit_bytes=VMEM_LIMIT),
         name='up',
     )(x, g, wr, wg, wu, choice_t)
 
 
-def run_down(tier, hid, x, gate, tab, wd):
+def run_late(act, late, wg, wu):
+    d_model = late.shape[1]
+    vm = pl.BlockSpec(memory_space=pltpu.VMEM)
+    hbm = pl.BlockSpec(memory_space=pltpu.HBM)
+    return pl.pallas_call(
+        late_kernel,
+        out_shape=jax.ShapeDtypeStruct((late.shape[0], 128), BF16),
+        in_specs=[pl.BlockSpec(memory_space=pltpu.SMEM), vm, hbm, hbm],
+        out_specs=vm,
+        scratch_shapes=[
+            pltpu.SMEM((64,), jnp.int32),
+            pltpu.VMEM((LATE_BUFS, d_model, 256), BF16),
+            pltpu.SemaphoreType.DMA((LATE_BUFS, 2)),
+        ],
+        compiler_params=pltpu.CompilerParams(vmem_limit_bytes=40 * 1024 * 1024),
+        name='late',
+    )(act, late, wg, wu)
+
+
+def run_down(tier, early, late, x, gate, tab, wd):
     rows_c, rows_n = TIERS[tier]
     tok, d_model = x.shape
     local = wd.shape[0]
     cw = d_model // 2 // DOWN_STEPS
-    slots = hid.shape[0]
+    slots = local * GROUPS * CAP
     vm = pl.BlockSpec(memory_space=pltpu.VMEM)
-    hbm = pl.BlockSpec(memory_space=pl.ANY)
+    hbm = pl.BlockSpec(memory_space=pltpu.HBM)
     sem = pltpu.SemaphoreType.DMA
     return pl.pallas_call(
         functools.partial(down_kernel, rows_c, rows_n),
         out_shape=jax.ShapeDtypeStruct(x.shape, BF16),
-        in_specs=[vm] * 4 + [hbm],
+        in_specs=[vm] * 5 + [hbm],
         out_specs=vm,
         scratch_shapes=[
+            pltpu.VMEM((slots, 128), BF16),
             pltpu.VMEM((DOWN_STEPS, 2, GROUPS, rows_c, cw), BF16),
             pltpu.VMEM((DOWN_STEPS, 2, GROUPS, rows_c, cw), BF16),
             pltpu.VMEM((DOWN_STEPS, rows_n, cw), BF16),
@@ -439,14 +506,15 @@
         ],
         compiler_params=pltpu.CompilerParams(collective_id=1 + tier, has_side_effects=True, vmem_limit_bytes=DOWN_VMEM[tier]),
         name='down%d' % rows_c,
-    )(hid, x, gate, tab, wd)
+    )(early, late, x, gate, tab, wd)
 
 
 def solution(mesh):
     row_spec = P(('dp', 'ep'), None)
 
     def device_step(resid_in, norm_scale, w_router, w_gate, w_up, w_down, choice):
-        hid, gate, tab, flag = run_up(resid_in, norm_scale, w_router, w_gate, w_up, choice.T)
-        return lax.switch(flag[0], [functools.partial(run_down, t) for t in range(len(TIERS))], hid, resid_in, gate, tab, w_down)
+        early, rows_late, gate, tab, act, flag = run_up(resid_in, norm_scale, w_router, w_gate, w_up, choice.T)
+        late = run_late(act, rows_late, w_gate, w_up)
+        return lax.switch(flag[0], [functools.partial(run_down, t) for t in range(len(TIERS))], early, late, resid_in, gate, tab, w_down)
 
     return jax.shard_map(device_step, mesh=mesh, in_specs=(row_spec, P(None), P(None, None), P('ep', None, 'tp'), P('ep', None, 'tp'), P('ep', 'tp', None), row_spec), out_specs=row_spec, check_vma=False)

time: 123 us -> 124 us (level); the launches traced: 123 us -> 125 us
  local copies, waits for them, and re-layouts: 1.23 us -> 4.13 us
    unnamed x3 -> x9, local copies, waits for them, and re-layouts: 1.23 us -> 4.13 us
    pallas_call x1 -> x2, Pallas kernels: 60.4 us -> 60.5 us  [the longest x1 46.4 us: run_up(): pl.pallas_call(up_kernel, out_shape=(jax.ShapeDtypeStruct((EARLY * 16, 12...]
where the time goes in v4:
time: 124 us; the launch traced here: 125 us
  Pallas kernels  121 us (98%)
  local copies, waits for them, and re-layouts  4.13 us (3%)
    pallas_call x1, Pallas kernels, run_down(): pl.pallas_call(functools.partial(down_kernel, rows_c, rows_n), out_shape=...  60.1 us
    pallas_call x1, Pallas kernels, run_up(): pl.pallas_call(up_kernel, out_shape=(jax.ShapeDtypeStruct((EARLY * 16, 12...  46.4 us
    pallas_call x1, Pallas kernels, run_late(): pl.pallas_call(late_kernel, out_shape=jax.ShapeDtypeStruct((late.shape[0]...  14.1 us
    unnamed x9, local copies, waits for them, and re-layouts  4.13 us

profile of v4, /device:TPU:0, one launch (start us, length us, event | category | flops | bytes accessed | tf_op | source)
XLA Modules:
  0.0 125.4 jit_solution(5872321023754657086)
XLA Ops:
  0.0 0.0 copy-start
  0.0 1.5 %copy-done = bf16[7168,128]{1,0:T(8,128)(2,1)S(1)} copy-done((bf16[7168,128]{1,0:T(8,128)(2,1)S(1)}, bf16[7168,128]{1,0:T(8,128)(2,1)}, u32[]{:S(2)}) %copy-start) | copy-done | bytes 1835032
  1.5 0.0 copy-start.1
  1.5 0.7 copy-done.1
  2.2 0.0 copy-start.2
  2.2 0.7 copy-done.2
  2.9 46.4 %up.1 = (bf16[288,128]{1,0:T(8,128)(2,1)S(1)}, bf16[224,7168]{1,0:T(8,128)(2,1)S(1)}, f32[128,2]{1,0:T(8,128)S(1)}, s32[4,8,128]{2,1,0:T(8,128)S(1)}, s32[1,128]{1,0:T(1,128)S(1)}, /*index=5*/s32[1]{0:T(128)}) custom-call(bf16[128,7168]{1,0:T(8,128)(2,1)} %x_ref.1, bf16[7168]{0:T(1024)(128)(2,1)S(1)} %copy-done.1, bf16[7168,128]{1,0:T(8,128)(2,1)S(1)} %copy-done, ...), custom_call_target="tpu_custom_call" | custom-call | tf_op jit(solution)/shard_map/up/pallas_call | solution.py:432
  49.8 0.0 copy-start.3
  49.9 14.1 %late.1 = bf16[224,128]{1,0:T(8,128)(2,1)S(1)} custom-call(s32[1,128]{1,0:T(1,128)S(1)} %get-tuple-element.52.act_ref, bf16[224,7168]{1,0:T(8,128)(2,1)S(1)} %get-tuple-element.53.late_ref, bf16[32,7168,128]{2,1,0:T(8,128)(2,1)} %wg_hbm.3, bf16[32,7168,128]{2,1,0:T(8,128)(2,1)} %wu_hbm.3), custom_call_target="tpu_custom_call" | custom-call | tf_op jit(solution)/shard_map/late/pallas_call | solution.py:463
  64.0 0.0 copy-done.3
  64.0 60.1 %conditional.1 = (bf16[128,7168]{1,0:T(8,128)(2,1)S(1)}) conditional(s32[]{:T(128)} %bitcast.1, (bf16[288,128]{1,0:T(8,128)(2,1)S(1)}, bf16[224,128]{1,0:T(8,128)(2,1)S(1)}, bf16[128,7168]{1,0:T(8,128)(2,1)S(1)}, f32[128,2]{1,0:T(8,128)S(1)}, s32[4,8,128]{2,1,0:T(8,128)S(1)}, /*index=5*/bf16[32,128,7168]{2,1,0:T(8,128)(2,1)}) %tuple.16, ...), branch_computations={%region_0.0_spmd, %region_1.0_spmd} | conditional | bytes 8 | solution.py:518
  64.0 60.1 %down64.1 = bf16[128,7168]{1,0:T(8,128)(2,1)S(1)} custom-call(bf16[288,128]{1,0:T(8,128)(2,1)S(1)} %get-tuple-element.32.early_ref, bf16[224,128]{1,0:T(8,128)(2,1)S(1)} %get-tuple-element.33.late_ref, bf16[128,7168]{1,0:T(8,128)(2,1)S(1)} %get-tuple-element.34.x_ref, f32[128,2]{1,0:T(8,128)S(1)} %get-tuple-element.35.gate_ref, ...), custom_call_target="tpu_custom_call" | custom-call | tf_op jit(solution)/shard_map/cond/branch_0_fun/down64/pallas_call | solution.py:487
  124.1 1.2 copy.15
Async XLA Ops:
  0.0 1.5 %copy-start = (bf16[7168,128]{1,0:T(8,128)(2,1)S(1)}, bf16[7168,128]{1,0:T(8,128)(2,1)}, u32[]{:S(2)}) copy-start(bf16[7168,128]{1,0:T(8,128)(2,1)} %wr_ref.1) | copy-start | bytes 5505028
  1.5 0.7 copy-start.1
  2.2 0.7 copy-start.2
  49.8 14.2 %copy-start.3 = (bf16[128,7168]{1,0:T(8,128)(2,1)S(1)}, bf16[128,7168]{1,0:T(8,128)(2,1)}, u32[]{:S(2)}) copy-start(bf16[128,7168]{1,0:T(8,128)(2,1)} %x_ref.1) | copy-start | bytes 5505028

commit v5 on v4

--- a/solution.py
+++ b/solution.py
@@ -16,10 +16,11 @@
 UP_STEPS = 14
 UP_BUFS = 6
 EARLY = 18
+AHEAD = 3
 LATE_BUFS = 6
 UP_LAG = 3
 DOWN_STEPS = 14
-DOWN_BUFS = 6
+DOWN_BUFS = 4
 DOWN_LAG = 2
 TIERS = ((64, 176), (128, 256))
 DOWN_VMEM = (46 * 1024 * 1024, 56 * 1024 * 1024)
@@ -67,7 +68,7 @@
                 out.append(pltpu.make_async_copy(w.at[0:EARLY, rows, :], wbuf.at[slot, :, h * cw:(h + 1) * cw, m * 128:(m + 1) * 128], w_sem.at[slot, h * 2 + m]))
         return out
 
-    for b in range(UP_BUFS):
+    for b in range(2):
         for c in weight_copies(b, b):
             c.start()
 
@@ -114,7 +115,10 @@
         own_copy(j).start()
         return carry
 
-    lax.fori_loop(0, steps, first_sends, 0)
+    lax.fori_loop(0, AHEAD, first_sends, 0)
+    for b in range(2, UP_BUFS):
+        for c in weight_copies(b, b):
+            c.start()
     ch_ref[ep] = choice_ref[...]
     acc_ref[...] = jnp.zeros_like(acc_ref)
     logit_ref[...] = jnp.zeros_like(logit_ref)
@@ -168,6 +172,10 @@
             y_copy(i).start()
             dx_copy(i).start()
 
+        @pl.when(i + AHEAD < steps)
+        def _():
+            first_sends(i + AHEAD, 0)
+
         @pl.when((i >= UP_LAG) & (i < steps + UP_LAG))
         def _():
             j = i - UP_LAG
@@ -298,7 +306,7 @@
             out.append(pltpu.make_async_copy(wd_hbm.at[:, :, cols], w2buf.at[slot, :, :, h * cw:(h + 1) * cw], w_sem.at[slot, h]))
         return out
 
-    for b in range(DOWN_BUFS):
+    for b in range(DOWN_BUFS - 2):
         for c in weight_copies(b, b):
             c.start()
 
@@ -375,12 +383,13 @@
                 send_ref[i, h] = jnp.dot(p_ref[...], qs_ref[:, h * cw:(h + 1) * cw], preferred_element_type=F32).astype(BF16).reshape(GROUPS, rows_c, cw)
             land_ref[i, :, ep] = send_ref[i, :, ep]
 
-            @pl.when(i + DOWN_BUFS < steps)
-            def _():
-                for c in weight_copies(i + DOWN_BUFS, slot):
-                    c.start()
             for n in range(3):
                 q_copy(i, n).start()
+
+            @pl.when(i + DOWN_BUFS - 2 < steps)
+            def _():
+                for c in weight_copies(i + DOWN_BUFS - 2, lax.rem(i + DOWN_BUFS - 2, DOWN_BUFS)):
+                    c.start()
 
         @pl.when((i >= DOWN_LAG) & (i < steps + DOWN_LAG))
         def _():

time: 124 us -> 122 us (0.984); the launches traced: 125 us -> 121 us
  Pallas kernels: 121 us -> 117 us
    pallas_call x1, Pallas kernels: 14.1 us -> 10 us  [run_late(): pl.pallas_call(late_kernel, out_shape=jax.ShapeDtypeStruct((late.shape[0]...]
where the time goes in v5:
time: 122 us; the launch traced here: 121 us
  Pallas kernels  117 us (96%)
  local copies, waits for them, and re-layouts  4.13 us (3%)
    pallas_call x1, Pallas kernels, run_down(): pl.pallas_call(functools.partial(down_kernel, rows_c, rows_n), out_shape=...  60.3 us
    pallas_call x1, Pallas kernels, run_up(): pl.pallas_call(up_kernel, out_shape=(jax.ShapeDtypeStruct((EARLY * 16, 12...  46.4 us
    pallas_call x1, Pallas kernels, run_late(): pl.pallas_call(late_kernel, out_shape=jax.ShapeDtypeStruct((late.shape[0]...  10 us
    unnamed x9, local copies, waits for them, and re-layouts  4.13 us

profile of v5, /device:TPU:0, one launch (start us, length us, event | category | flops | bytes accessed | tf_op | source)
XLA Modules:
  0.0 121.5 jit_solution(16003592925267317615)
XLA Ops:
  0.0 0.0 copy-start
  0.0 1.5 %copy-done = bf16[7168,128]{1,0:T(8,128)(2,1)S(1)} copy-done((bf16[7168,128]{1,0:T(8,128)(2,1)S(1)}, bf16[7168,128]{1,0:T(8,128)(2,1)}, u32[]{:S(2)}) %copy-start) | copy-done | bytes 1835032
  1.5 0.0 copy-start.1
  1.5 0.7 copy-done.1
  2.2 0.0 copy-start.2
  2.2 0.7 copy-done.2
  2.9 46.4 %up.1 = (bf16[288,128]{1,0:T(8,128)(2,1)S(1)}, bf16[224,7168]{1,0:T(8,128)(2,1)S(1)}, f32[128,2]{1,0:T(8,128)S(1)}, s32[4,8,128]{2,1,0:T(8,128)S(1)}, s32[1,128]{1,0:T(1,128)S(1)}, /*index=5*/s32[1]{0:T(128)}) custom-call(bf16[128,7168]{1,0:T(8,128)(2,1)} %x_ref.1, bf16[7168]{0:T(1024)(128)(2,1)S(1)} %copy-done.1, bf16[7168,128]{1,0:T(8,128)(2,1)S(1)} %copy-done, ...), custom_call_target="tpu_custom_call" | custom-call | tf_op jit(solution)/shard_map/up/pallas_call | solution.py:441
  49.9 0.0 copy-start.3
  49.9 10.0 %late.1 = bf16[224,128]{1,0:T(8,128)(2,1)S(1)} custom-call(s32[1,128]{1,0:T(1,128)S(1)} %get-tuple-element.52.act_ref, bf16[224,7168]{1,0:T(8,128)(2,1)S(1)} %get-tuple-element.53.late_ref, bf16[32,7168,128]{2,1,0:T(8,128)(2,1)} %wg_hbm.3, bf16[32,7168,128]{2,1,0:T(8,128)(2,1)} %wu_hbm.3), custom_call_target="tpu_custom_call" | custom-call | tf_op jit(solution)/shard_map/late/pallas_call | solution.py:472
  59.9 0.0 copy-done.3
  59.9 60.3 %conditional.1 = (bf16[128,7168]{1,0:T(8,128)(2,1)S(1)}) conditional(s32[]{:T(128)} %bitcast.1, (bf16[288,128]{1,0:T(8,128)(2,1)S(1)}, bf16[224,128]{1,0:T(8,128)(2,1)S(1)}, bf16[128,7168]{1,0:T(8,128)(2,1)S(1)}, f32[128,2]{1,0:T(8,128)S(1)}, s32[4,8,128]{2,1,0:T(8,128)S(1)}, /*index=5*/bf16[32,128,7168]{2,1,0:T(8,128)(2,1)}) %tuple.16, ...), branch_computations={%region_0.0_spmd, %region_1.0_spmd} | conditional | bytes 8 | solution.py:527
  59.9 60.3 %down64.1 = bf16[128,7168]{1,0:T(8,128)(2,1)S(1)} custom-call(bf16[288,128]{1,0:T(8,128)(2,1)S(1)} %get-tuple-element.32.early_ref, bf16[224,128]{1,0:T(8,128)(2,1)S(1)} %get-tuple-element.33.late_ref, bf16[128,7168]{1,0:T(8,128)(2,1)S(1)} %get-tuple-element.34.x_ref, f32[128,2]{1,0:T(8,128)S(1)} %get-tuple-element.35.gate_ref, ...), custom_call_target="tpu_custom_call" | custom-call | tf_op jit(solution)/shard_map/cond/branch_0_fun/down64/pallas_call | solution.py:496
  120.2 1.2 %copy.15 = bf16[128,7168]{1,0:T(8,128)(2,1)} copy(bf16[128,7168]{1,0:T(8,128)(2,1)S(1)} %get-tuple-element.56) | data formatting | bytes 3670016
Async XLA Ops:
  0.0 1.5 %copy-start = (bf16[7168,128]{1,0:T(8,128)(2,1)S(1)}, bf16[7168,128]{1,0:T(8,128)(2,1)}, u32[]{:S(2)}) copy-start(bf16[7168,128]{1,0:T(8,128)(2,1)} %wr_ref.1) | copy-start | bytes 5505028
  1.5 0.7 copy-start.1
  2.2 0.7 copy-start.2
  49.9 10.0 %copy-start.3 = (bf16[128,7168]{1,0:T(8,128)(2,1)S(1)}, bf16[128,7168]{1,0:T(8,128)(2,1)}, u32[]{:S(2)}) copy-start(bf16[128,7168]{1,0:T(8,128)(2,1)} %x_ref.1) | copy-start | bytes 5505028

commit v6 on v5

--- a/solution.py
+++ b/solution.py
@@ -13,17 +13,17 @@
 BF16 = jnp.bfloat16
 CAP = 4
 GROUPS = 4
-UP_STEPS = 14
-UP_BUFS = 6
+UP_STEPS = 7
+UP_BUFS = 3
 EARLY = 18
 AHEAD = 3
 LATE_BUFS = 6
-UP_LAG = 3
+UP_LAG = 2
 DOWN_STEPS = 14
 DOWN_BUFS = 4
 DOWN_LAG = 2
-TIERS = ((64, 176), (128, 256))
-DOWN_VMEM = (46 * 1024 * 1024, 56 * 1024 * 1024)
+TIERS = ((64, 176), (80, 192), (96, 224), (128, 256))
+DOWN_VMEM = (46 * 1024 * 1024, 48 * 1024 * 1024, 52 * 1024 * 1024, 56 * 1024 * 1024)
 VMEM_LIMIT = 48 * 1024 * 1024
 
 
@@ -95,8 +95,7 @@
     for n in range(3):
         choice_copy(n).start()
 
-    def own_copy(j):
-        return remote(u_ref.at[j, :, ep], u_ref.at[j, :, ep], own_s.at[j], own_r.at[j], twin)
+    own_copy = remote(u_ref.at[:, :, ep], u_ref.at[:, :, ep], own_s, own_r, twin)
 
     def x_copy(j):
         return remote(u_ref.at[j, tp, ep], u_ref.at[j, tp, ep], x_s.at[j], x_r.at[j], across)
@@ -112,10 +111,10 @@
 
     def first_sends(j, carry):
         x_copy(j).start()
-        own_copy(j).start()
         return carry
 
     lax.fori_loop(0, AHEAD, first_sends, 0)
+    own_copy.start()
     for b in range(2, UP_BUFS):
         for c in weight_copies(b, b):
             c.start()
@@ -189,7 +188,9 @@
             for h in range(2):
                 kr = pl.ds(pl.multiple_of(h * half + j * cw, cw), cw)
                 logit_ref[...] += jnp.dot(u_ref[j, h, ep], wr_ref[kr, :], preferred_element_type=F32)
-            own_copy(j).wait_recv()
+            @pl.when(j == 0)
+            def _():
+                own_copy.wait_recv()
             dx_copy(j).wait_recv()
             dy_copy(j).wait_recv()
             for h in range(2):
@@ -229,13 +230,13 @@
 
     def last_waits(j, carry):
         x_copy(j).wait_send()
-        own_copy(j).wait_send()
         y_copy(j).wait_send()
         dx_copy(j).wait_send()
         dy_copy(j).wait_send()
         return carry
 
     lax.fori_loop(0, steps, last_waits, 0)
+    own_copy.wait_send()
     for n in range(3):
         choice_copy(n).wait_send()
 
@@ -458,8 +459,8 @@
             pltpu.VMEM((UP_BUFS, EARLY, 2 * cw, 256), BF16),
             pltpu.VMEM((tok, 128), F32),
             pltpu.VMEM((GROUPS, 2, tok), jnp.int32),
-            sem((UP_BUFS, 4)), sem((3,)), sem((3,)),
-        ] + [sem((UP_STEPS,))] * 10,
+            sem((UP_BUFS, 4)), sem((3,)), sem((3,)), sem, sem,
+        ] + [sem((UP_STEPS,))] * 8,
         compiler_params=pltpu.CompilerParams(collective_id=0, has_side_effects=True, vmem_limit_bytes=VMEM_LIMIT),
         name='up',
     )(x, g, wr, wg, wu, choice_t)

time: 122 us -> 119 us (0.975); the launches traced: 121 us -> 117 us
  Pallas kernels: 117 us -> 112 us
    pallas_call x1, Pallas kernels: 46.4 us -> 42.2 us  [run_up(): pl.pallas_call(up_kernel, out_shape=(jax.ShapeDtypeStruct((EARLY * 16, 12...]
    pallas_call x1, Pallas kernels: 10 us -> 8.74 us  [run_late(): pl.pallas_call(late_kernel, out_shape=jax.ShapeDtypeStruct((late.shape[0]...]
where the time goes in v6:
time: 119 us; the launch traced here: 117 us
  Pallas kernels  112 us (94%)
  local copies, waits for them, and re-layouts  4.13 us (3%)
    pallas_call x1, Pallas kernels, run_down(): pl.pallas_call(functools.partial(down_kernel, rows_c, rows_n), out_shape=...  60.8 us
    pallas_call x1, Pallas kernels, run_up(): pl.pallas_call(up_kernel, out_shape=(jax.ShapeDtypeStruct((EARLY * 16, 12...  42.2 us
    pallas_call x1, Pallas kernels, run_late(): pl.pallas_call(late_kernel, out_shape=jax.ShapeDtypeStruct((late.shape[0]...  8.74 us
    unnamed x9, local copies, waits for them, and re-layouts  4.13 us

profile of v6, /device:TPU:0, one launch (start us, length us, event | category | flops | bytes accessed | tf_op | source)
XLA Modules:
  0.0 116.6 jit_solution(11562552081172063778)
XLA Ops:
  0.0 0.0 copy-start
  0.0 1.5 %copy-done = bf16[7168,128]{1,0:T(8,128)(2,1)S(1)} copy-done((bf16[7168,128]{1,0:T(8,128)(2,1)S(1)}, bf16[7168,128]{1,0:T(8,128)(2,1)}, u32[]{:S(2)}) %copy-start) | copy-done | bytes 1835032
  1.5 0.0 copy-start.1
  1.5 0.7 copy-done.1
  2.2 0.0 copy-start.2
  2.2 0.7 copy-done.2
  2.9 42.2 %up.1 = (bf16[288,128]{1,0:T(8,128)(2,1)S(1)}, bf16[224,7168]{1,0:T(8,128)(2,1)S(1)}, f32[128,2]{1,0:T(8,128)S(1)}, s32[4,8,128]{2,1,0:T(8,128)S(1)}, s32[1,128]{1,0:T(1,128)S(1)}, /*index=5*/s32[1]{0:T(128)}) custom-call(bf16[128,7168]{1,0:T(8,128)(2,1)} %x_ref.1, bf16[7168]{0:T(1024)(128)(2,1)S(1)} %copy-done.1, bf16[7168,128]{1,0:T(8,128)(2,1)S(1)} %copy-done, ...), custom_call_target="tpu_custom_call" | custom-call | tf_op jit(solution)/shard_map/up/pallas_call | solution.py:442
  45.7 0.0 copy-start.3
  45.7 8.7 %late.1 = bf16[224,128]{1,0:T(8,128)(2,1)S(1)} custom-call(s32[1,128]{1,0:T(1,128)S(1)} %get-tuple-element.90.act_ref, bf16[224,7168]{1,0:T(8,128)(2,1)S(1)} %get-tuple-element.91.late_ref, bf16[32,7168,128]{2,1,0:T(8,128)(2,1)} %wg_hbm.3, bf16[32,7168,128]{2,1,0:T(8,128)(2,1)} %wu_hbm.3), custom_call_target="tpu_custom_call" | custom-call | tf_op jit(solution)/shard_map/late/pallas_call | solution.py:473
  54.4 0.0 copy-done.3
  54.5 60.9 %conditional.1 = (bf16[128,7168]{1,0:T(8,128)(2,1)S(1)}) conditional(s32[]{:T(128)} %bitcast.1, (bf16[288,128]{1,0:T(8,128)(2,1)S(1)}, bf16[224,128]{1,0:T(8,128)(2,1)S(1)}, bf16[128,7168]{1,0:T(8,128)(2,1)S(1)}, f32[128,2]{1,0:T(8,128)S(1)}, s32[4,8,128]{2,1,0:T(8,128)S(1)}, ...), branch_computations={%region_0.0_spmd, %region_1.0_spmd, %region_2.0_spmd, %region_3.0_... | conditional | bytes 8 | solution.py:528
  54.5 60.8 %down64.1 = bf16[128,7168]{1,0:T(8,128)(2,1)S(1)} custom-call(bf16[288,128]{1,0:T(8,128)(2,1)S(1)} %get-tuple-element.56.early_ref, bf16[224,128]{1,0:T(8,128)(2,1)S(1)} %get-tuple-element.58.late_ref, bf16[128,7168]{1,0:T(8,128)(2,1)S(1)} %get-tuple-element.60.x_ref, f32[128,2]{1,0:T(8,128)S(1)} %get-tuple-element.61.gate_ref, ...), custom_call_target="tpu_custom_call" | custom-call | tf_op jit(solution)/shard_map/cond/branch_0_fun/down64/pallas_call | solution.py:497
  115.3 1.2 %copy.21 = bf16[128,7168]{1,0:T(8,128)(2,1)} copy(bf16[128,7168]{1,0:T(8,128)(2,1)S(1)} %get-tuple-element.94) | data formatting | bytes 3670016
Async XLA Ops:
  0.0 1.5 %copy-start = (bf16[7168,128]{1,0:T(8,128)(2,1)S(1)}, bf16[7168,128]{1,0:T(8,128)(2,1)}, u32[]{:S(2)}) copy-start(bf16[7168,128]{1,0:T(8,128)(2,1)} %wr_ref.1) | copy-start | bytes 5505028
  1.5 0.7 copy-start.1
  2.2 0.7 copy-start.2
  45.7 8.8 %copy-start.3 = (bf16[128,7168]{1,0:T(8,128)(2,1)S(1)}, bf16[128,7168]{1,0:T(8,128)(2,1)}, u32[]{:S(2)}) copy-start(bf16[128,7168]{1,0:T(8,128)(2,1)} %x_ref.1) | copy-start | bytes 5505028
